TPU v7x, 512 devices: a whole 4x4x16 slice. The times are simulated.
512 devices in a mesh: dimer: 128 (over x, z, core), rep: 4 (over y).
Axes of the slice: x: 4, y: 4, z: 16, core: 2. Of those that a mesh axis runs over, the one named last changes fastest.
Arguments:
- integrals: bfloat16 [4096, 256, 3, 128], P('dimer', 'rep'), may hold values from -0.375 to 0.375
- density: bfloat16 [4096, 256], P('dimer', 'rep'), may hold values from -6 to 6
- energy_terms: bfloat16 [4096, 256], P('dimer', 'rep'), may hold values from -0.005859375 to 0.005859375
- positions: float32 [3, 262144], P(None, ('dimer', 'rep')), may hold values from -0.01171875 to 0.01171875
- dimer_owners: int32 [4096, 2], P('dimer'), may hold values from 0 to 127, all different within a row; in each aligned block of 32 rows (0 to 31, 32 to 63, ...) at most 2 rows name the same one
- dimer_local: int32 [4096, 2], P('dimer'), may hold values from 0 to 31
Outputs:
- forces: float32 [3, 262144], P(None, ('dimer', 'rep'))
- energy: float32 [], replicated
- virial: float32 [], replicated
Inputs may be any that keep to these rules, and one draw needn't show every extreme that they name: `dimer_owners`: the two entries of a row differ. Among the 32 rows of one device no value stands more than 2 times, and some value stands exactly 2 times in some device's rows.
All inputs are finite; a program needn't handle non-finite values.
Results may differ from a plain program's by a relative error of at most 0.00045.
Values sent between devices are 32-bit elements; how exact they have to be, the bound alone decides.
No kernel may reach another device: no remote copies, remote signals or barrier semaphores. Data moves between devices by JAX's collectives and lax.ppermute only.
A program may use at most 64 MiB of HBM per device.

v0:
```python
import jax
import jax.numpy as jnp
from jax import lax
from jax.sharding import Mesh
from jax.sharding import PartitionSpec as P

FRAG_DEV = 32
DIMER = ("dimer_0", "dimer_1", "dimer_2")
DIMER_REP = ("dimer_0", "dimer_1", "dimer_2", "rep")


def in_one_piece(arrays, axis, split_dim, concat_dim, along):
    both = jnp.concatenate(arrays, axis=along)
    out, at, finished = (
        lax.all_to_all(both, axis, split_axis=split_dim, concat_axis=concat_dim, tiled=True),
        0,
        [],
    )
    for a in arrays:
        finished.append(lax.slice_in_dim(out, at, at + a.shape[along], axis=along))
        at += a.shape[along]
    return tuple(finished)


def split_up(array, dim, length):
    before, after = (array.shape[:dim], array.shape[dim + 1 :])
    return jnp.moveaxis(array.reshape(*before, length, -1, *after), dim, 0)


def sent_and_summed(array, axis, dim):
    length = lax.axis_size(axis)
    parts = lax.all_to_all(split_up(array, dim, length), axis, 0, 0, tiled=True)
    return jnp.sum(parts, axis=0)


def from_everyone(array, axis):
    copies = jnp.broadcast_to(array, (lax.axis_size(axis), *array.shape))
    return lax.all_to_all(copies, axis, split_axis=0, concat_axis=0, tiled=True)


def taken_together(array, axis):
    everything = from_everyone(array, axis)
    return jnp.sum(everything, axis=0)


def by_axis(array, axes):
    far, near = axes
    nearer = taken_together(array, near)
    return taken_together(nearer, far)


def packed_total(arrays, axis):
    ravelled, at, finished = (jnp.concatenate([a.reshape(-1) for a in arrays]), 0, [])
    subtotal = by_axis(ravelled, axis)
    for a in arrays:
        finished.append(subtotal[at : at + a.size].reshape(a.shape))
        at += a.size
    return tuple(finished)


def on_device(integrals, density, energy_terms, positions, dimer_owners, dimer_local):
    slots = integrals.shape[0]
    atoms = integrals.shape[3] // 2
    owner_count = lax.axis_size(DIMER)
    highest = lax.Precision.HIGHEST
    partial_value = jnp.einsum(
        "sk,skcb->scb", density, integrals, preferred_element_type=jnp.float32
    )
    energy_part = jnp.sum(density.astype(jnp.float32) * energy_terms.astype(jnp.float32))
    capacity = max(2, 4 * slots // owner_count)
    flat_owner = dimer_owners.reshape(-1)
    order = jnp.arange(2 * slots, dtype=jnp.int32)
    earlier = (flat_owner[:, None] == flat_owner[None, :]) & (order[None, :] < order[:, None])
    rank = jnp.sum(earlier.astype(jnp.int32), axis=1)
    target = flat_owner * capacity + rank
    route = (
        target[:, None] == jnp.arange(owner_count * capacity, dtype=jnp.int32)[None, :]
    ).astype(jnp.float32)
    send_blocks = jnp.einsum(
        "stn,scta->nca",
        route.reshape(slots, 2, -1),
        partial_value.reshape(slots, 3, 2, atoms),
        precision=highest,
    )
    local_hot = (
        dimer_local.reshape(-1)[:, None] == jnp.arange(FRAG_DEV, dtype=jnp.int32)[None, :]
    ).astype(jnp.float32)
    send_index = jnp.einsum("pn,pf->nf", route, local_hot, precision=highest)
    got_blocks, got_index = in_one_piece(
        (
            send_blocks.reshape(owner_count, capacity, 3 * atoms),
            send_index.reshape(owner_count, capacity, FRAG_DEV),
        ),
        DIMER,
        0,
        0,
        2,
    )
    lane = jnp.einsum(
        "nqf,nqca->cfa",
        got_index,
        got_blocks.reshape(owner_count, capacity, 3, atoms),
        precision=highest,
    )
    forces = sent_and_summed(lane, "rep", 1).reshape(3, -1)
    virial_part = -jnp.sum(positions * forces) / 3.0
    energy, virial = packed_total(
        (energy_part, virial_part), (("dimer_0", "dimer_1"), ("dimer_2", "rep"))
    )
    return (forces, energy, virial)


def solution(mesh):
    split = Mesh(
        mesh.devices.reshape(4, 16, 2, mesh.shape["rep"]), ("dimer_0", "dimer_1", "dimer_2", "rep")
    )
    placed = (
        P(DIMER, "rep", None, None),
        P(DIMER, "rep"),
        P(DIMER, "rep"),
        P(None, DIMER_REP),
        P(DIMER, None),
        P(DIMER, None),
    )
    return jax.shard_map(
        on_device,
        mesh=split,
        in_specs=placed,
        out_specs=(P(None, DIMER_REP), P(), P()),
        check_vma=False,
    )
```

profile of v0, /device:TPU:1, one launch (start us, length us, event | category | flops | bytes accessed | tf_op | source)
XLA Modules:
  0.0 90.2 jit_solution(8337708323437842122)
XLA Ops:
  0.6 0.0 copy-start
  0.7 0.9 copy.62
  1.5 0.1 eq.62
  1.6 0.2 convert_reduce_fusion
  1.8 0.1 reduce_sum.57
  1.9 0.8 copy.65
  2.7 0.1 eq.77
  2.8 0.1 copy.63
  2.9 0.7 multiply_add_fusion.1
  3.6 0.0 copy-done
  3.6 1.1 %fusion.7 = f32[32,1,3,128]{3,1,2,0:T(1,128)S(1)} fusion(bf16[32,64,3,128]{3,1,2,0:T(8,128)(2,1)S(1)} %copy-done, bf16[32,64,1,1]{1,0,2,3:T(8,128)(2,1)} %bitcast.42), kind=kOutput, calls=%fused_computation.16 | convolution fusion | flops 1572864 | bytes 1626112 | tf_op jit(solution)/shard_map/sk,skcb->scb/dot_general | solution.py:66
  4.7 0.1 reshape.67
  4.8 0.1 copy.64
  4.9 0.1 reshape.78
  5.0 0.3 fusion
  5.3 0.1 copy.67
  5.3 0.0 copy-start.1
  5.4 0.0 copy-start.3
  5.4 0.3 convolution_bitcast_fusion
  5.7 0.0 copy-start.4
  5.7 0.1 copy.68
  5.9 42.6 %all_to_all.22 = f32[128,2,224]{2,1,0:T(2,128)S(1)} all-to-all(f32[128,2,224]{2,1,0:T(2,128)S(1)} %copy.68), channel_id=1, replica_groups=mesh['dimer_0'=4,'dimer_1'=16,'dimer_2'=2,'rep'=4] {'dimer_0','dimer_1',..., dimensions={0} | all-to-all | bytes 458752 | tf_op jit(solution)/shard_map/all_to_all | solution.py:15
  48.5 0.2 slice.17
  48.7 0.1 copy.81
  48.7 0.1 copy.69
  48.9 0.3 convolution_bitcast_fusion.1
  49.2 0.7 reshape.83
  49.9 4.2 %all-to-all-start.1 = ((f32[4,1,1536]{2,1,0:T(1,128)}), f32[4,1,1536]{2,1,0:T(1,128)S(1)}, u32[]{:S(2)}, u32[]{:S(2)}) async-start(f32[4,1,1536]{2,1,0:T(1,128)} %reshape.83), calls=%async_computation.1 | async-start | bytes 49152 | tf_op jit(solution)/shard_map/all_to_all | solution.py:32
  54.1 0.0 copy-done.1
  54.1 0.0 copy-done.3
  54.1 0.6 multiply_reduce_fusion
  54.7 3.6 %all-to-all-done.1 = f32[4,1,1536]{2,1,0:T(1,128)S(1)} async-done(((f32[4,1,1536]{2,1,0:T(1,128)}), f32[4,1,1536]{2,1,0:T(1,128)S(1)}, u32[]{:S(2)}, u32[]{:S(2)}) %all-to-all-start.1) | async-done | bytes 24608 | tf_op jit(solution)/shard_map/all_to_all | solution.py:32
  58.4 0.5 broadcast.21
  58.9 0.7 reduce.2
  59.6 0.1 reshape.84
  59.7 0.1 reshape.71
  59.8 0.0 copy-done.4
  59.8 0.0 copy-start.2
  59.8 0.6 multiply_reduce_fusion.1
  61.0 0.7 pad_maximum_fusion.1
  61.8 10.6 %all_to_all.23 = f32[8,1,2]{2,1,0:T(1,128)S(1)} all-to-all(f32[8,1,2]{2,1,0:T(1,128)S(1)} %broadcast_in_dim.4), channel_id=1, replica_groups=mesh['dimer_0'=4,'dimer_1'=16,'dimer_2'=2,'rep'=4] {'dimer_2','rep'}, dimensions={0} | all-to-all | bytes 128 | tf_op jit(solution)/shard_map/all_to_all | solution.py:38
  72.4 17.1 %all_to_all.24 = f32[64,1,2]{2,1,0:T(1,128)S(1)} all-to-all(f32[64,1,2]{2,1,0:T(1,128)S(1)} %broadcast_in_dim.5), channel_id=1, replica_groups=mesh['dimer_0'=4,'dimer_1'=16,'dimer_2'=2,'rep'=4] {'dimer_0','dimer_1'}, dimensions={0} | all-to-all | bytes 1024 | tf_op jit(solution)/shard_map/all_to_all | solution.py:38
  89.5 0.1 reduce_sum.62
  89.6 0.6 fusion.10
  90.2 0.0 copy-done.2
  (9 shorter events, 0.1 us)
Async XLA Ops:
  0.6 3.0 %copy-start = (bf16[32,64,3,128]{3,1,2,0:T(8,128)(2,1)S(1)}, bf16[32,64,3,128]{3,1,2,0:T(8,128)(2,1)}, u32[]{:S(2)}) copy-start(bf16[32,64,3,128]{3,1,2,0:T(8,128)(2,1)} %param.6) | copy-start | bytes 4718596
  5.3 48.8 %copy-start.1 = (bf16[32,64]{1,0:T(8,128)(2,1)S(1)}, bf16[32,64]{1,0:T(8,128)(2,1)}, u32[]{:S(2)}) copy-start(bf16[32,64]{1,0:T(8,128)(2,1)} %param.7) | copy-start | bytes 12292
  5.4 48.8 %copy-start.3 = (bf16[32,64]{1,0:T(8,128)(2,1)S(1)}, bf16[32,64]{1,0:T(8,128)(2,1)}, u32[]{:S(2)}) copy-start(bf16[32,64]{1,0:T(8,128)(2,1)} %param.8) | copy-start | bytes 12292
  5.7 54.1 %copy-start.4 = (f32[3,512]{1,0:T(4,128)S(1)}, f32[3,512]{1,0:T(4,128)}, u32[]{:S(2)}) copy-start(f32[3,512]{1,0:T(4,128)} %param.9) | copy-start | bytes 18436
  49.9 8.4 %all-to-all-start.1 = ((f32[4,1,1536]{2,1,0:T(1,128)}), f32[4,1,1536]{2,1,0:T(1,128)S(1)}, u32[]{:S(2)}, u32[]{:S(2)}) async-start(f32[4,1,1536]{2,1,0:T(1,128)} %reshape.83), calls=%async_computation.1 | async-start | bytes 49152 | tf_op jit(solution)/shard_map/all_to_all | solution.py:32
  59.8 30.4 %copy-start.2 = (f32[3,512]{1,0:T(4,128)}, f32[3,512]{1,0:T(4,128)S(1)}, u32[]{:S(2)}) copy-start(f32[3,512]{1,0:T(4,128)S(1)} %reshape.71) | copy-start | bytes 18436
where the time goes:
time: 90.6 us; the launch traced here: 90.2 us
  blocking collectives  70.3 us (78%)
  local copies, waits for them, and re-layouts  4.99 us (6%)
  starting transfers between devices  4.18 us (5%)
  other arithmetic  3.66 us (4%)
  waiting for transfers between devices  3.65 us (4%)
  matrix products  2.03 us (2%)
  between operations  1.41 us (2%)
    all_to_all x1, blocking collectives, in_one_piece(): lax.all_to_all(both, axis, split_axis=split_dim, concat_axis=concat_dim,...  42.6 us
    all_to_all x2, blocking collectives, from_everyone(): return lax.all_to_all(copies, axis, split_axis=0, concat_axis=0, tiled=True)  27.7 us
    all_to_all x1, starting transfers between devices, sent_and_summed(): parts = lax.all_to_all(split_up(array, dim, length), axis, 0, 0, tiled=True)  4.18 us
    all_to_all x1, waiting for transfers between devices, sent_and_summed(): parts = lax.all_to_all(split_up(array, dim, length), axis, 0, 0, tiled=True)  3.65 us
    unnamed x15, local copies, waits for them, and re-layouts  2.51 us
  transfers between devices with their start and end apart: 1, of which 1 were waited for; matrix products, arithmetic and copies ran while one was open for 1% of the time, Pallas kernels for 0%

commit v1 on v0

v1 whole, which is shorter than its diff:
```python
import jax
import jax.numpy as jnp
from jax import lax
from jax.experimental import pallas as pl
from jax.experimental.pallas import tpu as pltpu
from jax.sharding import Mesh
from jax.sharding import PartitionSpec as P

X, Z, C, Y = 4, 16, 2, 4
XC = X * C
PLANE = XC * Y
AT = 64
SLOTS = 32
LOC, NRG = 192, 193
DIMER = ("x", "z", "c")
ALL = ("x", "z", "c", "y")
f32, bf16, i32 = jnp.float32, jnp.bfloat16, jnp.int32


def iota(shape, dim):
    return lax.broadcasted_iota(i32, shape, dim)


def split(v):
    hi = v.astype(bf16)
    return hi, (v - hi.astype(f32)).astype(bf16)


def dot(a, b, dims=((1,), (0,))):
    return lax.dot_general(a, b, (dims, ((), ())), preferred_element_type=f32)


def swap(v):
    return pltpu.roll(v, AT, 1)


def pair(a, b):
    return jnp.where(iota(a.shape, 1) < AT, a, b)


def send_kernel(h_ints, h_dens, h_terms, h_own, h_loc, h_pos, out, pos_out, *scratch):
    ints, dens, terms, own, loc, pos, sems = scratch
    sources = (h_own, h_loc, h_pos, h_dens, h_terms, h_ints)
    copies = [
        pltpu.make_async_copy(a, b, sems.at[i])
        for i, (a, b) in enumerate(zip(sources, (own, loc, pos, dens, terms, ints)))
    ]
    for copy in copies:
        copy.start()
    for copy in copies:
        copy.wait()

    d = dens[...].astype(f32)
    dd = jnp.concatenate([d, d], axis=1)
    row, half = iota(dd.shape, 0), iota(dd.shape, 1) // AT
    diag = jnp.concatenate(
        [jnp.where(row == 2 * j + half, dd, 0.0).astype(bf16) for j in range(SLOTS // 2)], axis=1
    )
    g0, g1, g2 = (dot(diag, ints[:, c].reshape(SLOTS * AT, 2 * AT)) for c in range(3))
    energy = jnp.sum(d * terms[...].astype(f32))

    o = jnp.concatenate([own[0:1], own[1:2]] * 2, axis=1)
    z, xc = (o >> 1) & (Z - 1), (o >> 5) * C + (o & 1)
    e = (iota((Z * XC, 4 * SLOTS), 0) == z * XC + xc).astype(bf16)
    p, q = iota((4 * SLOTS, 4 * SLOTS), 0), iota((4 * SLOTS, 4 * SLOTS), 1)
    before = ((p < 2 * SLOTS) & (p < q % (2 * SLOTS))).astype(bf16)
    count = dot(e, before)
    e3, count3 = e.astype(f32).reshape(Z, 1, XC, 4 * SLOTS), count.reshape(Z, 1, XC, 4 * SLOTS)
    route = jnp.concatenate([jnp.where(count3 == r, e3, 0.0) for r in (0.0, 1.0)], axis=1)
    route = route.reshape(Z * 2 * XC, 4 * SLOTS).astype(bf16)

    same = iota((SLOTS, SLOTS), 0) == iota((SLOTS, SLOTS), 1)
    places = [
        jnp.sum(jnp.where(same, loc[t : t + 1].astype(f32), 0.0), axis=1, keepdims=True)
        for t in range(2)
    ]
    places = [jnp.broadcast_to(v, (SLOTS, 2 * AT)) for v in places]
    rows = jnp.concatenate(
        [
            jnp.concatenate([pair(g0, swap(g1)), pair(g2, places[0])], axis=1),
            jnp.concatenate([pair(swap(g0), g1), pair(swap(g2), places[1])], axis=1),
        ],
        axis=0,
    )
    sent = dot(route, jnp.concatenate(split(rows), axis=0))
    sent = jnp.where(iota(sent.shape, 1) == NRG, energy, sent)
    out[...] = sent.reshape(Z, 2 * XC, 4 * AT)

    lines = []
    for f in range(8):
        w = pos[:, 2 * AT * (f // 2) : 2 * AT * (f // 2 + 1)]
        s = swap(w)
        a, b = (w, s) if f % 2 == 0 else (s, w)
        zero = jnp.zeros((1, 2 * AT), f32)
        lines.append(
            jnp.concatenate([pair(a[0:1], b[1:2]), pair(a[2:3], zero)], axis=1)
        )
    block = jnp.concatenate(lines, axis=0)
    pos_out[...] = jnp.broadcast_to(block[None], pos_out.shape)


def lane_kernel(got, pos, out):
    v = got[...].reshape(Z * 2 * XC, 4 * AT)
    n = (Z * 2 * XC, PLANE * 8)
    place = v[:, LOC : LOC + 1].astype(i32)
    q = iota(n, 1)
    pick = ((q >> 5) == (iota(n, 0) & (XC - 1))) & ((q & 31) == place)
    pick = pick.astype(f32).astype(bf16)
    hi, lo = split(v)
    lane = dot(pick, hi, ((0,), (0,))) + dot(pick, lo, ((0,), (0,)))
    at = iota(lane.shape, 1)
    virial = -jnp.sum(jnp.where(at < LOC, lane * pos[...].reshape(lane.shape), 0.0)) / 3.0
    first = (iota(v.shape, 0) & (2 * XC - 1)) == 0
    energy = jnp.sum(jnp.where(first & (iota(v.shape, 1) == NRG), v, 0.0)) / Z
    lane = jnp.where(at == LOC, virial, jnp.where(at == NRG, energy, lane))
    out[...] = lane.reshape(PLANE, 8, 4 * AT)


def force_kernel(got, forces, scalars):
    s = jnp.sum(got[...], axis=0)
    u, w = s[:, : 2 * AT], s[:, 2 * AT :]
    su, sw = swap(u), swap(w)
    for k in range(4):
        a, b = slice(2 * k, 2 * k + 1), slice(2 * k + 1, 2 * k + 2)
        cols = slice(2 * AT * k, 2 * AT * (k + 1))
        forces[0:1, cols] = pair(u[a], su[b])
        forces[1:2, cols] = pair(su[a], u[b])
        forces[2:3, cols] = pair(w[a], sw[b])
    scalars[...] = jnp.broadcast_to(w[0:1][None], scalars.shape)


VM = pl.BlockSpec(memory_space=pltpu.VMEM)
HBM = pl.BlockSpec(memory_space=pltpu.HBM)


def call(kernel, outs, n, flops, scratch=(), where=VM):
    return pl.pallas_call(
        kernel,
        out_shape=outs,
        in_specs=[where] * n,
        scratch_shapes=scratch,
        out_specs=jax.tree.map(lambda _: VM, outs),
        cost_estimate=pl.CostEstimate(flops=flops, bytes_accessed=1 << 20, transcendentals=0),
        compiler_params=pltpu.CompilerParams(vmem_limit_bytes=16 << 20),
    )


def arr(*shape):
    return jax.ShapeDtypeStruct(shape, f32)


def on_device(integrals, density, energy_terms, positions, dimer_owners, dimer_local):
    args = (
        jnp.transpose(integrals, (0, 2, 1, 3)),
        density,
        energy_terms,
        dimer_owners.T,
        dimer_local.T,
        positions,
    )
    scratch = [pltpu.VMEM(a.shape, a.dtype) for a in args] + [pltpu.SemaphoreType.DMA((6,))]
    outs = (arr(Z, 2 * XC, 4 * AT), arr(PLANE, 8, 4 * AT))
    sent, pos = call(send_kernel, outs, 6, 4_000_000, scratch, HBM)(
        *(pltpu.with_memory_space_constraint(a, pltpu.HBM) for a in args)
    )
    got = lax.all_to_all(sent, "z", 0, 0, tiled=True)
    pos = lax.all_to_all(pos, ("x", "c", "y"), 0, 0, tiled=True)
    lane = call(lane_kernel, arr(PLANE, 8, 4 * AT), 2, 4_000_000)(got, pos)
    parts = lax.all_to_all(lane, ("x", "c", "y"), 0, 0, tiled=True)
    forces, scalars = call(force_kernel, (arr(3, 8 * AT), arr(Z, 1, 2 * AT)), 1, 1_000_000)(parts)
    totals = jnp.sum(lax.all_to_all(scalars, "z", 0, 0, tiled=True), axis=(0, 1))
    return forces, totals[NRG - 2 * AT], totals[LOC - 2 * AT]


def solution(mesh):
    split_mesh = Mesh(mesh.devices.reshape(X, Z, C, Y), ALL)
    placed = (
        P(DIMER, "y", None, None),
        P(DIMER, "y"),
        P(DIMER, "y"),
        P(None, ALL),
        P(DIMER, None),
        P(DIMER, None),
    )
    return jax.shard_map(
        on_device,
        mesh=split_mesh,
        in_specs=placed,
        out_specs=(P(None, ALL), P(), P()),
        check_vma=False,
    )
```

time: 90.6 us -> 84.5 us (0.933)
  blocking collectives: 70.3 us -> 79.6 us
  local copies, waits for them, and re-layouts: 4.99 us -> 0.59 us
  starting transfers between devices: 4.18 us -> 0 us
  waiting for transfers between devices: 3.65 us -> 0 us
  other arithmetic: 3.66 us -> 0.03 us
  Pallas kernels: 0 us -> 3.37 us
  matrix products: 2.03 us -> 0 us
    all_to_all x3 -> x4, blocking collectives: 70.3 us -> 79.6 us  [the longest x1 27.3 us: on_device(): got = lax.all_to_all(sent, 'z', 0, 0, tiled=True)]
    all_to_all x1 -> x0, starting transfers between devices: 4.18 us -> none  [sent_and_summed(): parts = lax.all_to_all(split_up(array, dim, length), axis, 0, 0, tiled=True)]
    all_to_all x1 -> x0, waiting for transfers between devices: 3.65 us -> none  [sent_and_summed(): parts = lax.all_to_all(split_up(array, dim, length), axis, 0, 0, tiled=True)]
    pallas_call x0 -> x3, Pallas kernels: none -> 3.37 us  [the longest x1 2.19 us: on_device(): call(send_kernel, outs, 6, 4000000, scratch, HBM)]
    unnamed x15 -> x0, local copies, waits for them, and re-layouts: 2.51 us -> none
    dot_general x4 -> x0, matrix products: 2.03 us -> none  [the longest x1 1.07 us: on_device(): jnp.einsum('sk,skcb->scb', density, integrals, preferred_element_type=jnp...]
    reduce_sum x6 -> x1, other arithmetic: 1.51 us -> 0.03 us  [on_device(): jnp.sum(lax.all_to_all(scalars, 'z', 0, 0, tiled=True), axis=(0, 1))]
  transfers between devices with their start and end apart: 1 -> 0, of which waited for: 1 -> 0; matrix products, arithmetic and copies ran while one was open for 1% -> 0% of each run, Pallas kernels for 0% -> 0%
where the time goes in v1:
time: 84.5 us; the launch traced here: 84.2 us
  blocking collectives  79.6 us (94%)
  Pallas kernels  3.37 us (4%)
    all_to_all x1, blocking collectives, on_device(): got = lax.all_to_all(sent, 'z', 0, 0, tiled=True)  27.3 us
    all_to_all x1, blocking collectives, on_device(): pos = lax.all_to_all(pos, ('x', 'c', 'y'), 0, 0, tiled=True)  18.4 us
    all_to_all x1, blocking collectives, on_device(): parts = lax.all_to_all(lane, ('x', 'c', 'y'), 0, 0, tiled=True)  17.5 us
    all_to_all x1, blocking collectives, on_device(): lax.all_to_all(scalars, 'z', 0, 0, tiled=True)  16.4 us
    pallas_call x1, Pallas kernels, on_device(): call(send_kernel, outs, 6, 4000000, scratch, HBM)  2.19 us

profile of v1, /device:TPU:1, one launch (start us, length us, event | category | flops | bytes accessed | tf_op | source)
XLA Modules:
  0.0 84.2 jit_solution(6208515740500344715)
XLA Ops:
  0.6 2.2 %shard_map.85 = (f32[16,16,256]{2,1,0:T(8,128)S(1)}, f32[32,8,256]{2,1,0:T(8,128)S(1)}) custom-call(bf16[32,3,64,128]{3,2,1,0:T(8,128)(2,1)} %bitcast.5, bf16[32,64]{1,0:T(8,128)(2,1)} %h_dens.1, bf16[32,64]{1,0:T(8,128)(2,1)} %h_terms.1, s32[2,32]{1,0:T(2,128)} %bitcast.6, s32[2,32]{1,0:T(2,128)} %bitcast.7, f32[3,512]{1,0:T(4,128)} %h_pos.1), custom_call_target="tpu_custom_call" | custom-call | flops 4000000 | bytes 1048576 | tf_op jit(solution)/shard_map/pallas_call | solution.py:163
  2.8 18.4 %all_to_all.20.pos = f32[32,8,256]{2,1,0:T(8,128)S(1)} all-to-all(f32[32,8,256]{2,1,0:T(8,128)S(1)} %get-tuple-element.8), channel_id=1, replica_groups=mesh['x'=4,'z'=16,'c'=2,'y'=4] {'x','c','y'}, dimensions={0} | all-to-all | bytes 524288 | tf_op jit(solution)/shard_map/all_to_all | solution.py:167
  21.2 27.3 %all_to_all.21.got = f32[16,16,256]{2,1,0:T(8,128)S(1)} all-to-all(f32[16,16,256]{2,1,0:T(8,128)S(1)} %get-tuple-element.7), channel_id=1, replica_groups=mesh['x'=4,'z'=16,'c'=2,'y'=4] {'z'}, dimensions={0} | all-to-all | bytes 524288 | tf_op jit(solution)/shard_map/all_to_all | solution.py:166
  48.5 0.5 shard_map.86
  49.0 17.5 %all_to_all.22.got = f32[32,8,256]{2,1,0:T(8,128)S(1)} all-to-all(f32[32,8,256]{2,1,0:T(8,128)S(1)} %shard_map.86), channel_id=1, replica_groups=mesh['x'=4,'z'=16,'c'=2,'y'=4] {'x','c','y'}, dimensions={0} | all-to-all | bytes 524288 | tf_op jit(solution)/shard_map/all_to_all | solution.py:169
  66.5 0.7 shard_map.87
  67.2 16.4 %all_to_all.23 = f32[16,1,128]{2,1,0:T(1,128)S(1)} all-to-all(f32[16,1,128]{2,1,0:T(1,128)S(1)} %get-tuple-element.10), channel_id=1, replica_groups=mesh['x'=4,'z'=16,'c'=2,'y'=4] {'z'}, dimensions={0} | all-to-all | bytes 16384 | tf_op jit(solution)/shard_map/all_to_all | solution.py:171
  83.6 0.6 fusion
  (1 shorter events, 0.0 us)

commit v2 on v1

v2 whole, which is shorter than its diff:
```python
import jax
import jax.numpy as jnp
from jax import lax
from jax.experimental import pallas as pl
from jax.experimental.pallas import tpu as pltpu
from jax.sharding import Mesh
from jax.sharding import PartitionSpec as P

X, Z, C, Y = 4, 16, 2, 4
XC = X * C
PLANE = XC * Y
AT = 64
W = 128
SLOTS = 32
Q = 48
PLACE, POS, SCALAR = 2 * Q, 98, 127
DIMER = ("x", "z", "c")
ALL = ("x", "z", "c", "y")
f32, bf16, i32 = jnp.float32, jnp.bfloat16, jnp.int32


def iota(shape, dim):
    return lax.broadcasted_iota(i32, shape, dim)


def split(v):
    hi = v.astype(bf16)
    return hi, (v - hi.astype(f32)).astype(bf16)


def dot(a, b, dims=((1,), (0,))):
    return lax.dot_general(a, b, (dims, ((), ())), preferred_element_type=f32)


def turn(v, by):
    by %= W
    return pltpu.roll(v, by, 1) if by else v


def pair(a, b):
    return jnp.where(iota(a.shape, 1) < AT, a, b)


def window(v0, v1, first, count, to):
    lane = iota(v0.shape, 1)
    inside = (lane >= to) & (lane < to + count)
    if first + count <= W:
        v = turn(v0, to - first)
    elif first >= W:
        v = turn(v1, to - first)
    else:
        v = jnp.where(lane < to + W - first, turn(v0, to - first), turn(v1, to - first))
    return jnp.where(inside, v, 0.0)


def send_kernel(h_ints, h_dens, h_terms, h_own, h_loc, h_pos, out, *scratch):
    ints, dens, terms, own, loc, pos, sems = scratch
    sources = (h_own, h_loc, h_pos, h_dens, h_terms, h_ints)
    copies = [
        pltpu.make_async_copy(a, b, sems.at[i])
        for i, (a, b) in enumerate(zip(sources, (own, loc, pos, dens, terms, ints)))
    ]
    for copy in copies:
        copy.start()
    for copy in copies[:-1]:
        copy.wait()

    o = jnp.concatenate([own[0:1], own[1:2]] * 2, axis=1)
    z, xc = (o >> 1) & (Z - 1), (o >> 5) * C + (o & 1)
    e = (iota((XC * Z, W), 0) == xc * Z + z).astype(f32).astype(bf16)
    p, q = iota((W, W), 0), iota((W, W), 1)
    before = ((p < 2 * SLOTS) & (p < q % (2 * SLOTS))).astype(f32).astype(bf16)
    count = dot(e, before)
    rank = (iota((XC * Z, W), 1) >= 2 * SLOTS).astype(f32)
    route = jnp.where(count == rank, e.astype(f32), 0.0).astype(bf16)
    same = iota((SLOTS, SLOTS), 0) == iota((SLOTS, SLOTS), 1)
    places = [
        jnp.sum(jnp.where(same, loc[t : t + 1].astype(f32), 0.0), axis=1, keepdims=True)
        for t in range(2)
    ]
    place = jnp.concatenate([jnp.broadcast_to(v, (SLOTS, W)) for v in places], axis=0)

    lines = []
    for f in range(8):
        w = pos[:, W * (f // 2) : W * (f // 2 + 1)]
        s = turn(w, AT)
        a, b = (w, s) if f % 2 == 0 else (s, w)
        lines.append((pair(a[0:1], b[1:2]), a[2:3]))
    x0, x1 = (jnp.concatenate([line[i] for line in lines], axis=0) for i in range(2))

    d = dens[...].astype(f32)
    energy = jnp.sum(d * terms[...].astype(f32))
    dd = jnp.concatenate([d, d], axis=1)
    row, half = iota(dd.shape, 0), iota(dd.shape, 1) // AT
    diag = jnp.concatenate(
        [jnp.where(row == 2 * j + half, dd, 0.0).astype(bf16) for j in range(SLOTS // 2)], axis=1
    )

    copies[-1].wait()
    g0, g1, g2 = (dot(diag, ints[:, c].reshape(SLOTS * AT, 2 * AT)) for c in range(3))
    v0 = jnp.concatenate([pair(g0, turn(g1, AT)), pair(turn(g0, AT), g1)], axis=0)
    v1 = jnp.concatenate([g2, turn(g2, AT)], axis=0)

    lane = iota((2 * SLOTS, W), 1)
    shares = []
    for y in range(Y):
        rows = [
            jnp.where(lane == PLACE + r, place, window(v0, v1, Q * y, Q, Q * r)) for r in range(2)
        ]
        shares.append(jnp.concatenate(rows, axis=0))
    hi, lo = split(jnp.concatenate(shares, axis=1))
    sent = dot(route, hi) + dot(route, lo)
    at = iota((2 * 8, W), 1)
    for y in range(Y):
        extra = jnp.concatenate(
            [window(x0, x1, Q * y + Q // 2 * h, Q // 2, POS) for h in range(2)], axis=0
        )
        extra = jnp.where(at == SCALAR, energy, extra)
        share = sent[:, W * y : W * (y + 1)].reshape(XC, Z, W)
        for k in range(XC):
            out[k * Y + y] = jnp.where(at < POS, share[k], extra)


def me():
    return lax.axis_index("x") * C + lax.axis_index("c")


def turn_kernel(got, out, pos):
    for k in range(XC):
        s = (got[k * Y] + got[k * Y + 1]) + (got[k * Y + 2] + got[k * Y + 3])
        out[:, k, :] = s
    mine = got[pl.ds(me() * Y, Y)]
    a, b = mine[:, :8].reshape(SLOTS, W), mine[:, 8:].reshape(SLOTS, W)
    a, b = turn(a, -POS), turn(b, Q // 2 - POS)
    lane = iota(a.shape, 1)
    pos[...] = jnp.where(lane < Q // 2, a, jnp.where(lane < Q, b, 0.0))


def block_kernel(got, pos, out):
    v = got[...].reshape(Z * XC, W)
    lane = iota(v.shape, 1)
    f = iota((Z * XC, SLOTS), 1).astype(f32) * Y
    picks, datas = [], []
    for r in range(2):
        picks.append((v[:, PLACE + r : PLACE + r + 1] == f).astype(f32).astype(bf16))
        datas.append(jnp.where(lane < Q, turn(v, -Q * r), 0.0))
    pick = jnp.concatenate(picks, axis=0)
    hi, lo = split(jnp.concatenate(datas, axis=0))
    block = dot(pick, hi, ((0,), (0,))) + dot(pick, lo, ((0,), (0,)))
    virial = -jnp.sum(block * pos[...]) / 3.0
    energy = jnp.sum(jnp.where(lane == SCALAR, v, 0.0)) / (Z * PLANE)
    at = iota(block.shape, 1)
    block = jnp.where(at == SCALAR, energy, jnp.where(at == SCALAR - 1, virial, block))
    for k in range(XC):
        out[k * Y : (k + 1) * Y] = block.reshape(Y, 8, W)


def force_kernel(got, forces, scalars):
    total = jnp.sum(got[:, 0:1, :], axis=0)
    scalars[...] = jnp.broadcast_to(total[None], scalars.shape)
    mine = got[pl.ds(me() * Y, Y)]
    lane = iota((8, W), 1)
    m1, m2 = turn(mine[1], Q), turn(mine[2], 2 * Q)
    u = jnp.where(lane < Q, mine[0], jnp.where(lane < 2 * Q, m1, m2))
    w = jnp.where(lane < 3 * Q - W, m2, turn(mine[3], 3 * Q - W))
    su, sw = turn(u, AT), turn(w, AT)
    for k in range(4):
        a, b = slice(2 * k, 2 * k + 1), slice(2 * k + 1, 2 * k + 2)
        cols = slice(W * k, W * (k + 1))
        forces[0:1, cols] = pair(u[a], su[b])
        forces[1:2, cols] = pair(su[a], u[b])
        forces[2:3, cols] = pair(w[a], sw[b])


VM = pl.BlockSpec(memory_space=pltpu.VMEM)
HBM = pl.BlockSpec(memory_space=pltpu.HBM)


def call(kernel, outs, n, scratch=(), where=VM):
    return pl.pallas_call(
        kernel,
        out_shape=outs,
        in_specs=[where] * n,
        out_specs=jax.tree.map(lambda _: VM, outs),
        scratch_shapes=scratch,
        compiler_params=pltpu.CompilerParams(vmem_limit_bytes=16 << 20),
    )


def arr(*shape):
    return jax.ShapeDtypeStruct(shape, f32)


def exchange(v, axes):
    return lax.all_to_all(v, axes, 0, 0, tiled=True)


def on_device(integrals, density, energy_terms, positions, dimer_owners, dimer_local):
    args = (
        jnp.transpose(integrals, (0, 2, 1, 3)),
        density,
        energy_terms,
        dimer_owners.T,
        dimer_local.T,
        positions,
    )
    scratch = [pltpu.VMEM(a.shape, a.dtype) for a in args] + [pltpu.SemaphoreType.DMA((6,))]
    args = (pltpu.with_memory_space_constraint(a, pltpu.HBM) for a in args)
    v = call(send_kernel, arr(PLANE, Z, W), 6, scratch, HBM)(*args)
    v = exchange(v, ("x", "c", "y"))
    v, pos = call(turn_kernel, (arr(Z, XC, W), arr(SLOTS, W)), 1)(v)
    v = exchange(v, "z")
    v = call(block_kernel, arr(PLANE, 8, W), 2)(v, pos)
    v = exchange(v, ("x", "c", "y"))
    forces, v = call(force_kernel, (arr(3, 8 * AT), arr(Z, 1, W)), 1)(v)
    totals = jnp.sum(exchange(v, "z"), axis=(0, 1))
    return forces, totals[SCALAR], totals[SCALAR - 1]


def solution(mesh):
    split_mesh = Mesh(mesh.devices.reshape(X, Z, C, Y), ALL)
    placed = (
        P(DIMER, "y", None, None),
        P(DIMER, "y"),
        P(DIMER, "y"),
        P(None, ALL),
        P(DIMER, None),
        P(DIMER, None),
    )
    return jax.shard_map(
        on_device,
        mesh=split_mesh,
        in_specs=placed,
        out_specs=(P(None, ALL), P(), P()),
        check_vma=False,
    )
```

time: 84.5 us -> 75.4 us (0.89)
  blocking collectives: 79.6 us -> 70.3 us
    all_to_all x4, blocking collectives: 79.6 us -> 70.3 us  [exchange(): return lax.all_to_all(v, axes, 0, 0, tiled=True)]
    pallas_call x3 -> x4, Pallas kernels: 3.37 us -> 3.48 us  [the longest x1 2.23 us: on_device(): v = call(send_kernel, arr(PLANE, Z, W), 6, scratch, HBM)(*args)]
where the time goes in v2:
time: 75.4 us; the launch traced here: 75.1 us
  blocking collectives  70.3 us (93%)
  Pallas kernels  3.48 us (5%)
    all_to_all x4, blocking collectives, exchange(): return lax.all_to_all(v, axes, 0, 0, tiled=True)  70.3 us
    pallas_call x1, Pallas kernels, on_device(): v = call(send_kernel, arr(PLANE, Z, W), 6, scratch, HBM)(*args)  2.23 us

profile of v2, /device:TPU:1, one launch (start us, length us, event | category | flops | bytes accessed | tf_op | source)
XLA Modules:
  0.0 75.1 jit_solution(7667093718217012561)
XLA Ops:
  0.6 2.2 %shard_map.85 = f32[32,16,128]{2,1,0:T(8,128)S(1)} custom-call(bf16[32,3,64,128]{3,2,1,0:T(8,128)(2,1)} %bitcast.5, bf16[32,64]{1,0:T(8,128)(2,1)} %h_dens.1, bf16[32,64]{1,0:T(8,128)(2,1)} %h_terms.1, s32[2,32]{1,0:T(2,128)} %bitcast.6, s32[2,32]{1,0:T(2,128)} %bitcast.7, f32[3,512]{1,0:T(4,128)} %h_pos.1), custom_call_target="tpu_custom_call" | custom-call | tf_op jit(solution)/shard_map/pallas_call | solution.py:209
  2.9 18.4 %all_to_all.20.got = f32[32,16,128]{2,1,0:T(8,128)S(1)} all-to-all(f32[32,16,128]{2,1,0:T(8,128)S(1)} %shard_map.85), channel_id=1, replica_groups=mesh['x'=4,'z'=16,'c'=2,'y'=4] {'x','c','y'}, dimensions={0} | all-to-all | bytes 524288 | tf_op jit(solution)/shard_map/all_to_all | solution.py:195
  21.2 0.1 shard_map.86
  21.3 25.1 %all_to_all.21.got = f32[16,8,128]{2,1,0:T(8,128)S(1)} all-to-all(f32[16,8,128]{2,1,0:T(8,128)S(1)} %get-tuple-element.7), channel_id=1, replica_groups=mesh['x'=4,'z'=16,'c'=2,'y'=4] {'z'}, dimensions={0} | all-to-all | bytes 131072 | tf_op jit(solution)/shard_map/all_to_all | solution.py:195
  46.4 0.4 shard_map.87
  46.8 13.1 %all_to_all.22.got = f32[32,8,128]{2,1,0:T(8,128)S(1)} all-to-all(f32[32,8,128]{2,1,0:T(8,128)S(1)} %shard_map.87), channel_id=1, replica_groups=mesh['x'=4,'z'=16,'c'=2,'y'=4] {'x','c','y'}, dimensions={0} | all-to-all | bytes 262144 | tf_op jit(solution)/shard_map/all_to_all | solution.py:195
  59.9 0.8 %shard_map.88 = (f32[3,512]{1,0:T(4,128)}, f32[16,1,128]{2,1,0:T(1,128)S(1)}) custom-call(f32[32,8,128]{2,1,0:T(8,128)S(1)} %all_to_all.22.got), custom_call_target="tpu_custom_call" | custom-call | tf_op jit(solution)/shard_map/pallas_call | solution.py:215
  60.6 13.8 %all_to_all.23 = f32[16,1,128]{2,1,0:T(1,128)S(1)} all-to-all(f32[16,1,128]{2,1,0:T(1,128)S(1)} %get-tuple-element.10), channel_id=1, replica_groups=mesh['x'=4,'z'=16,'c'=2,'y'=4] {'z'}, dimensions={0} | all-to-all | bytes 16384 | tf_op jit(solution)/shard_map/all_to_all | solution.py:195
  74.5 0.6 fusion
  (1 shorter events, 0.0 us)

commit v3 on v2

--- a/solution.py
+++ b/solution.py
@@ -14,6 +14,10 @@
 SLOTS = 32
 Q = 48
 PLACE, POS, SCALAR = 2 * Q, 98, 127
+X0, C0, Y0, Z0 = 2, 1, 2, 8
+ZS = [(Z0 + k) % Z for k in range(Z)]
+YS = [(Y0 + k) % Y for k in range(Y)]
+XCS = [(X0 + i) % X * C + (C0 + j) % C for i in range(X) for j in range(C)]
 DIMER = ("x", "z", "c")
 ALL = ("x", "z", "c", "y")
 f32, bf16, i32 = jnp.float32, jnp.bfloat16, jnp.int32
@@ -66,7 +70,8 @@
         copy.wait()
 
     o = jnp.concatenate([own[0:1], own[1:2]] * 2, axis=1)
-    z, xc = (o >> 1) & (Z - 1), (o >> 5) * C + (o & 1)
+    z = ((o >> 1) - Z0) & (Z - 1)
+    xc = (((o >> 5) - X0) & (X - 1)) * C + ((o & 1) ^ C0)
     e = (iota((XC * Z, W), 0) == xc * Z + z).astype(f32).astype(bf16)
     p, q = iota((W, W), 0), iota((W, W), 1)
     before = ((p < 2 * SLOTS) & (p < q % (2 * SLOTS))).astype(f32).astype(bf16)
@@ -118,19 +123,20 @@
         extra = jnp.where(at == SCALAR, energy, extra)
         share = sent[:, W * y : W * (y + 1)].reshape(XC, Z, W)
         for k in range(XC):
-            out[k * Y + y] = jnp.where(at < POS, share[k], extra)
+            out[k * Y + YS.index(y)] = jnp.where(at < POS, share[k], extra)
 
 
 def me():
-    return lax.axis_index("x") * C + lax.axis_index("c")
+    return ((lax.axis_index("x") - X0) & (X - 1)) * C + (lax.axis_index("c") ^ C0)
 
 
 def turn_kernel(got, out, pos):
     for k in range(XC):
         s = (got[k * Y] + got[k * Y + 1]) + (got[k * Y + 2] + got[k * Y + 3])
         out[:, k, :] = s
-    mine = got[pl.ds(me() * Y, Y)]
-    a, b = mine[:, :8].reshape(SLOTS, W), mine[:, 8:].reshape(SLOTS, W)
+    mine = [got[me() * Y + YS.index(y)] for y in range(Y)]
+    a = jnp.concatenate([m[:8] for m in mine], axis=0)
+    b = jnp.concatenate([m[8:] for m in mine], axis=0)
     a, b = turn(a, -POS), turn(b, Q // 2 - POS)
     lane = iota(a.shape, 1)
     pos[...] = jnp.where(lane < Q // 2, a, jnp.where(lane < Q, b, 0.0))
@@ -151,14 +157,15 @@
     energy = jnp.sum(jnp.where(lane == SCALAR, v, 0.0)) / (Z * PLANE)
     at = iota(block.shape, 1)
     block = jnp.where(at == SCALAR, energy, jnp.where(at == SCALAR - 1, virial, block))
-    for k in range(XC):
-        out[k * Y : (k + 1) * Y] = block.reshape(Y, 8, W)
+    for k in range(PLANE):
+        y = YS[k % Y]
+        out[k] = block[8 * y : 8 * (y + 1)]
 
 
 def force_kernel(got, forces, scalars):
     total = jnp.sum(got[:, 0:1, :], axis=0)
     scalars[...] = jnp.broadcast_to(total[None], scalars.shape)
-    mine = got[pl.ds(me() * Y, Y)]
+    mine = [got[me() * Y + YS.index(y)] for y in range(Y)]
     lane = iota((8, W), 1)
     m1, m2 = turn(mine[1], Q), turn(mine[2], 2 * Q)
     u = jnp.where(lane < Q, mine[0], jnp.where(lane < 2 * Q, m1, m2))
@@ -191,8 +198,13 @@
     return jax.ShapeDtypeStruct(shape, f32)
 
 
-def exchange(v, axes):
-    return lax.all_to_all(v, axes, 0, 0, tiled=True)
+def over_z(v):
+    return lax.all_to_all(v, "z", 0, 0, axis_index_groups=[ZS], tiled=True)
+
+
+def over_plane(v):
+    order = [xc * Y + y for xc in XCS for y in YS]
+    return lax.all_to_all(v, ("x", "c", "y"), 0, 0, axis_index_groups=[order], tiled=True)
 
 
 def on_device(integrals, density, energy_terms, positions, dimer_owners, dimer_local):
@@ -207,13 +219,13 @@
     scratch = [pltpu.VMEM(a.shape, a.dtype) for a in args] + [pltpu.SemaphoreType.DMA((6,))]
     args = (pltpu.with_memory_space_constraint(a, pltpu.HBM) for a in args)
     v = call(send_kernel, arr(PLANE, Z, W), 6, scratch, HBM)(*args)
-    v = exchange(v, ("x", "c", "y"))
+    v = over_plane(v)
     v, pos = call(turn_kernel, (arr(Z, XC, W), arr(SLOTS, W)), 1)(v)
-    v = exchange(v, "z")
+    v = over_z(v)
     v = call(block_kernel, arr(PLANE, 8, W), 2)(v, pos)
-    v = exchange(v, ("x", "c", "y"))
+    v = over_plane(v)
     forces, v = call(force_kernel, (arr(3, 8 * AT), arr(Z, 1, W)), 1)(v)
-    totals = jnp.sum(exchange(v, "z"), axis=(0, 1))
+    totals = jnp.sum(over_z(v), axis=(0, 1))
     return forces, totals[SCALAR], totals[SCALAR - 1]
 
 

time: 75.4 us -> 65.3 us (0.87)
  blocking collectives: 70.3 us -> 60 us
    all_to_all x4, blocking collectives: 70.3 us -> 60 us  [the longest x2 30.5 us: over_z(): return lax.all_to_all(v, 'z', 0, 0, axis_index_groups=[ZS], tiled=True)]
where the time goes in v3:
time: 65.3 us; the launch traced here: 64.8 us
  blocking collectives  60 us (92%)
  Pallas kernels  3.48 us (5%)
    all_to_all x2, blocking collectives, over_z(): return lax.all_to_all(v, 'z', 0, 0, axis_index_groups=[ZS], tiled=True)  30.5 us
    all_to_all x2, blocking collectives, over_plane(): lax.all_to_all(v, ('x', 'c', 'y'), 0, 0, axis_index_groups=[order], tiled...  29.5 us
    pallas_call x1, Pallas kernels, on_device(): v = call(send_kernel, arr(PLANE, Z, W), 6, scratch, HBM)(*args)  2.23 us

profile of v3, /device:TPU:1, one launch (start us, length us, event | category | flops | bytes accessed | tf_op | source)
XLA Modules:
  0.0 64.8 jit_solution(10350786736017961210)
XLA Ops:
  0.6 2.2 %shard_map.85 = f32[32,16,128]{2,1,0:T(8,128)S(1)} custom-call(bf16[32,3,64,128]{3,2,1,0:T(8,128)(2,1)} %bitcast.5, bf16[32,64]{1,0:T(8,128)(2,1)} %h_dens.1, bf16[32,64]{1,0:T(8,128)(2,1)} %h_terms.1, s32[2,32]{1,0:T(2,128)} %bitcast.6, s32[2,32]{1,0:T(2,128)} %bitcast.7, f32[3,512]{1,0:T(4,128)} %h_pos.1), custom_call_target="tpu_custom_call" | custom-call | tf_op jit(solution)/shard_map/pallas_call | solution.py:221
  2.9 17.3 %all_to_all.20.got = f32[32,16,128]{2,1,0:T(8,128)S(1)} all-to-all(f32[32,16,128]{2,1,0:T(8,128)S(1)} %shard_map.85), channel_id=1, replica_groups={{262,263,260,261,258,259,256,257,390,391,388,389,386,387,384,385,6,7,4,..., dimensions={0} | all-to-all | bytes 524288 | tf_op jit(solution)/shard_map/all_to_all | solution.py:207
  20.2 0.1 shard_map.86
  20.3 17.5 %all_to_all.21.got = f32[16,8,128]{2,1,0:T(8,128)S(1)} all-to-all(f32[16,8,128]{2,1,0:T(8,128)S(1)} %get-tuple-element.7), channel_id=1, replica_groups={{64,72,80,88,96,104,112,120,0,8,16,24,32,40,48,56},{65,73,81,89,97,105,..., dimensions={0} | all-to-all | bytes 131072 | tf_op jit(solution)/shard_map/all_to_all | solution.py:202
  37.8 0.4 shard_map.87
  38.2 12.2 %all_to_all.22.got = f32[32,8,128]{2,1,0:T(8,128)S(1)} all-to-all(f32[32,8,128]{2,1,0:T(8,128)S(1)} %shard_map.87), channel_id=1, replica_groups={{262,263,260,261,258,259,256,257,390,391,388,389,386,387,384,385,6,7,4,..., dimensions={0} | all-to-all | bytes 262144 | tf_op jit(solution)/shard_map/all_to_all | solution.py:207
  50.4 0.8 %shard_map.88 = (f32[3,512]{1,0:T(4,128)}, f32[16,1,128]{2,1,0:T(1,128)S(1)}) custom-call(f32[32,8,128]{2,1,0:T(8,128)S(1)} %all_to_all.22.got), custom_call_target="tpu_custom_call" | custom-call | tf_op jit(solution)/shard_map/pallas_call | solution.py:227
  51.1 13.0 %all_to_all.23 = f32[16,1,128]{2,1,0:T(1,128)S(1)} all-to-all(f32[16,1,128]{2,1,0:T(1,128)S(1)} %get-tuple-element.10), channel_id=1, replica_groups={{64,72,80,88,96,104,112,120,0,8,16,24,32,40,48,56},{65,73,81,89,97,105,..., dimensions={0} | all-to-all | bytes 16384 | tf_op jit(solution)/shard_map/all_to_all | solution.py:202
  64.2 0.6 fusion
  (1 shorter events, 0.0 us)

commit v4 on v3

--- a/solution.py
+++ b/solution.py
@@ -13,6 +13,7 @@
 W = 128
 SLOTS = 32
 Q = 48
+PARTS = 4
 PLACE, POS, SCALAR = 2 * Q, 98, 127
 X0, C0, Y0, Z0 = 2, 1, 2, 8
 ZS = [(Z0 + k) % Z for k in range(Z)]
@@ -59,14 +60,13 @@
 
 def send_kernel(h_ints, h_dens, h_terms, h_own, h_loc, h_pos, out, *scratch):
     ints, dens, terms, own, loc, pos, sems = scratch
-    sources = (h_own, h_loc, h_pos, h_dens, h_terms, h_ints)
-    copies = [
-        pltpu.make_async_copy(a, b, sems.at[i])
-        for i, (a, b) in enumerate(zip(sources, (own, loc, pos, dens, terms, ints)))
-    ]
+    part = SLOTS // PARTS
+    pairs = [(h_dens, dens), (h_own, own), (h_loc, loc), (h_pos, pos), (h_terms, terms)]
+    pairs += [(h_ints.at[pl.ds(part * i, part)], ints.at[pl.ds(part * i, part)]) for i in range(PARTS)]
+    copies = [pltpu.make_async_copy(a, b, sems.at[i]) for i, (a, b) in enumerate(pairs)]
     for copy in copies:
         copy.start()
-    for copy in copies[:-1]:
+    for copy in copies[:-PARTS]:
         copy.wait()
 
     o = jnp.concatenate([own[0:1], own[1:2]] * 2, axis=1)
@@ -101,8 +101,12 @@
         [jnp.where(row == 2 * j + half, dd, 0.0).astype(bf16) for j in range(SLOTS // 2)], axis=1
     )
 
-    copies[-1].wait()
-    g0, g1, g2 = (dot(diag, ints[:, c].reshape(SLOTS * AT, 2 * AT)) for c in range(3))
+    g = jnp.zeros((SLOTS, 3 * W), f32)
+    for i in range(PARTS):
+        copies[i - PARTS].wait()
+        rows = [ints[pl.ds(part * i, part), c].reshape(part * AT, W) for c in range(3)]
+        g += dot(diag[:, part * AT * i : part * AT * (i + 1)], jnp.concatenate(rows, axis=1))
+    g0, g1, g2 = (g[:, W * c : W * (c + 1)] for c in range(3))
     v0 = jnp.concatenate([pair(g0, turn(g1, AT)), pair(turn(g0, AT), g1)], axis=0)
     v1 = jnp.concatenate([g2, turn(g2, AT)], axis=0)
 
@@ -157,15 +161,24 @@
     energy = jnp.sum(jnp.where(lane == SCALAR, v, 0.0)) / (Z * PLANE)
     at = iota(block.shape, 1)
     block = jnp.where(at == SCALAR, energy, jnp.where(at == SCALAR - 1, virial, block))
+    lower = turn(pltpu.roll(block, SLOTS - 4, 0), Q)
+    block = jnp.where((at < Q) | (at >= 2 * Q), block, lower)
     for k in range(PLANE):
         y = YS[k % Y]
-        out[k] = block[8 * y : 8 * (y + 1)]
-
-
-def force_kernel(got, forces, scalars):
+        out[k] = block[8 * y : 8 * y + 4]
+
+
+def scalar_kernel(got, scalars):
     total = jnp.sum(got[:, 0:1, :], axis=0)
     scalars[...] = jnp.broadcast_to(total[None], scalars.shape)
+
+
+def force_kernel(got, scalars, forces, energy, virial):
+    total = jnp.sum(scalars[...], axis=0)
+    energy[0] = total[0, SCALAR]
+    virial[0] = total[0, SCALAR - 1]
     mine = [got[me() * Y + YS.index(y)] for y in range(Y)]
+    mine = [jnp.concatenate([m, turn(m, -Q)], axis=0) for m in mine]
     lane = iota((8, W), 1)
     m1, m2 = turn(mine[1], Q), turn(mine[2], 2 * Q)
     u = jnp.where(lane < Q, mine[0], jnp.where(lane < 2 * Q, m1, m2))
@@ -181,15 +194,17 @@
 
 VM = pl.BlockSpec(memory_space=pltpu.VMEM)
 HBM = pl.BlockSpec(memory_space=pltpu.HBM)
-
-
-def call(kernel, outs, n, scratch=(), where=VM):
+SM = pl.BlockSpec(memory_space=pltpu.SMEM)
+
+
+def call(kernel, outs, n, scratch=(), where=VM, spaces=None):
     return pl.pallas_call(
         kernel,
         out_shape=outs,
         in_specs=[where] * n,
-        out_specs=jax.tree.map(lambda _: VM, outs),
+        out_specs=spaces or jax.tree.map(lambda _: VM, outs),
         scratch_shapes=scratch,
+        cost_estimate=pl.CostEstimate(flops=20_000_000, bytes_accessed=1 << 18, transcendentals=0),
         compiler_params=pltpu.CompilerParams(vmem_limit_bytes=16 << 20),
     )
 
@@ -216,17 +231,18 @@
         dimer_local.T,
         positions,
     )
-    scratch = [pltpu.VMEM(a.shape, a.dtype) for a in args] + [pltpu.SemaphoreType.DMA((6,))]
+    scratch = [pltpu.VMEM(a.shape, a.dtype) for a in args] + [pltpu.SemaphoreType.DMA((5 + PARTS,))]
     args = (pltpu.with_memory_space_constraint(a, pltpu.HBM) for a in args)
     v = call(send_kernel, arr(PLANE, Z, W), 6, scratch, HBM)(*args)
     v = over_plane(v)
     v, pos = call(turn_kernel, (arr(Z, XC, W), arr(SLOTS, W)), 1)(v)
     v = over_z(v)
-    v = call(block_kernel, arr(PLANE, 8, W), 2)(v, pos)
+    v = call(block_kernel, arr(PLANE, 4, W), 2)(v, pos)
     v = over_plane(v)
-    forces, v = call(force_kernel, (arr(3, 8 * AT), arr(Z, 1, W)), 1)(v)
-    totals = jnp.sum(over_z(v), axis=(0, 1))
-    return forces, totals[SCALAR], totals[SCALAR - 1]
+    scalars = over_z(call(scalar_kernel, arr(Z, 1, W), 1)(v))
+    outs = (arr(3, 8 * AT), arr(1), arr(1))
+    forces, energy, virial = call(force_kernel, outs, 2, spaces=(VM, SM, SM))(v, scalars)
+    return forces, energy.reshape(()), virial.reshape(())
 
 
 def solution(mesh):

time: 65.3 us -> 64.5 us (0.988)
    pallas_call x2 -> x3, Pallas kernels: 1.16 us -> 1.34 us  [the longest x1 0.83 us: on_device(): call(force_kernel, outs, 2, spaces=(VM, SM, SM))(v, scalars)]
where the time goes in v4:
time: 64.5 us; the launch traced here: 63.9 us
  blocking collectives  59.5 us (92%)
  Pallas kernels  3.69 us (6%)
    all_to_all x2, blocking collectives, over_z(): return lax.all_to_all(v, 'z', 0, 0, axis_index_groups=[ZS], tiled=True)  30.5 us
    all_to_all x2, blocking collectives, over_plane(): lax.all_to_all(v, ('x', 'c', 'y'), 0, 0, axis_index_groups=[order], tiled...  29 us
    pallas_call x1, Pallas kernels, on_device(): v = call(send_kernel, arr(PLANE, Z, W), 6, scratch, HBM)(*args)  2.26 us

profile of v4, /device:TPU:1, one launch (start us, length us, event | category | flops | bytes accessed | tf_op | source)
XLA Modules:
  0.0 63.9 jit_solution(2199126296088440226)
XLA Ops:
  0.6 2.3 %shard_map.85 = f32[32,16,128]{2,1,0:T(8,128)S(1)} custom-call(bf16[32,3,64,128]{3,2,1,0:T(8,128)(2,1)} %bitcast.5, bf16[32,64]{1,0:T(8,128)(2,1)} %h_dens.1, bf16[32,64]{1,0:T(8,128)(2,1)} %h_terms.1, s32[2,32]{1,0:T(2,128)} %bitcast.6, s32[2,32]{1,0:T(2,128)} %bitcast.7, f32[3,512]{1,0:T(4,128)} %h_pos.1), custom_call_target="tpu_custom_call" | custom-call | flops 20000000 | bytes 262144 | tf_op jit(solution)/shard_map/pallas_call | solution.py:236
  2.9 17.3 %all_to_all.20.got = f32[32,16,128]{2,1,0:T(8,128)S(1)} all-to-all(f32[32,16,128]{2,1,0:T(8,128)S(1)} %shard_map.85), channel_id=1, replica_groups={{262,263,260,261,258,259,256,257,390,391,388,389,386,387,384,385,6,7,4,..., dimensions={0} | all-to-all | bytes 524288 | tf_op jit(solution)/shard_map/all_to_all | solution.py:222
  20.2 0.1 shard_map.86
  20.3 17.5 %all_to_all.21.got = f32[16,8,128]{2,1,0:T(8,128)S(1)} all-to-all(f32[16,8,128]{2,1,0:T(8,128)S(1)} %get-tuple-element.8), channel_id=1, replica_groups={{64,72,80,88,96,104,112,120,0,8,16,24,32,40,48,56},{65,73,81,89,97,105,..., dimensions={0} | all-to-all | bytes 131072 | tf_op jit(solution)/shard_map/all_to_all | solution.py:217
  37.8 0.5 shard_map.87
  38.3 11.7 %all_to_all.22.got = f32[32,4,128]{2,1,0:T(4,128)S(1)} all-to-all(f32[32,4,128]{2,1,0:T(4,128)S(1)} %shard_map.87), channel_id=1, replica_groups={{262,263,260,261,258,259,256,257,390,391,388,389,386,387,384,385,6,7,4,..., dimensions={0} | all-to-all | bytes 131072 | tf_op jit(solution)/shard_map/all_to_all | solution.py:222
  50.0 13.0 %all_to_all.23.scalars = f32[16,1,128]{2,1,0:T(1,128)S(1)} all-to-all(f32[16,1,128]{2,1,0:T(1,128)S(1)} %shard_map.88), channel_id=1, replica_groups={{64,72,80,88,96,104,112,120,0,8,16,24,32,40,48,56},{65,73,81,89,97,105,..., dimensions={0} | all-to-all | bytes 16384 | tf_op jit(solution)/shard_map/all_to_all | solution.py:217
  63.0 0.8 %shard_map.89 = (f32[3,512]{1,0:T(4,128)}, f32[1]{0:T(128)}, f32[1]{0:T(128)}) custom-call(f32[32,4,128]{2,1,0:T(4,128)S(1)} %all_to_all.22.got, f32[16,1,128]{2,1,0:T(1,128)S(1)} %all_to_all.23.scalars), custom_call_target="tpu_custom_call" | custom-call | flops 20000000 | bytes 262144 | tf_op jit(solution)/shard_map/pallas_call | solution.py:244
  (1 shorter events, 0.0 us)

commit v5 on v4

--- a/solution.py
+++ b/solution.py
@@ -14,7 +14,7 @@
 SLOTS = 32
 Q = 48
 PARTS = 4
-PLACE, POS, SCALAR = 2 * Q, 98, 127
+PLACE, SCALAR = Q, 127
 X0, C0, Y0, Z0 = 2, 1, 2, 8
 ZS = [(Z0 + k) % Z for k in range(Z)]
 YS = [(Y0 + k) % Y for k in range(Y)]
@@ -70,20 +70,16 @@
         copy.wait()
 
     o = jnp.concatenate([own[0:1], own[1:2]] * 2, axis=1)
+    f = jnp.concatenate([loc[0:1], loc[1:2]] * 2, axis=1)
     z = ((o >> 1) - Z0) & (Z - 1)
     xc = (((o >> 5) - X0) & (X - 1)) * C + ((o & 1) ^ C0)
-    e = (iota((XC * Z, W), 0) == xc * Z + z).astype(f32).astype(bf16)
-    p, q = iota((W, W), 0), iota((W, W), 1)
-    before = ((p < 2 * SLOTS) & (p < q % (2 * SLOTS))).astype(f32).astype(bf16)
-    count = dot(e, before)
-    rank = (iota((XC * Z, W), 1) >= 2 * SLOTS).astype(f32)
-    route = jnp.where(count == rank, e.astype(f32), 0.0).astype(bf16)
-    same = iota((SLOTS, SLOTS), 0) == iota((SLOTS, SLOTS), 1)
-    places = [
-        jnp.sum(jnp.where(same, loc[t : t + 1].astype(f32), 0.0), axis=1, keepdims=True)
-        for t in range(2)
-    ]
-    place = jnp.concatenate([jnp.broadcast_to(v, (SLOTS, W)) for v in places], axis=0)
+    f = ((((f >> 3) - Y0) & (Y - 1)) << 3) + (f & 7)
+    row, col = iota((2 * SLOTS, W), 0), iota((2 * SLOTS, W), 1)
+    key = ((z * 8 + xc) * SLOTS + f) * (2 * SLOTS) + (col[:1] & (2 * SLOTS - 1))
+    key_of = jnp.sum(jnp.where(row == col, key.astype(f32), 0.0), axis=1, keepdims=True)
+    turn_of = jnp.sum((key_of < key.astype(f32)).astype(f32), axis=0, keepdims=True).astype(i32)
+    route = (row == (turn_of & 7) * 8 + (turn_of >> 3)).astype(f32).astype(bf16)
+    place = (key_of.astype(i32) >> 6).astype(f32)
 
     lines = []
     for f in range(8):
@@ -101,71 +97,64 @@
         [jnp.where(row == 2 * j + half, dd, 0.0).astype(bf16) for j in range(SLOTS // 2)], axis=1
     )
 
-    g = jnp.zeros((SLOTS, 3 * W), f32)
-    for i in range(PARTS):
-        copies[i - PARTS].wait()
-        rows = [ints[pl.ds(part * i, part), c].reshape(part * AT, W) for c in range(3)]
-        g += dot(diag[:, part * AT * i : part * AT * (i + 1)], jnp.concatenate(rows, axis=1))
-    g0, g1, g2 = (g[:, W * c : W * (c + 1)] for c in range(3))
+    for copy in copies[-PARTS:]:
+        copy.wait()
+    g0, g1, g2 = (dot(diag, ints[:, c].reshape(SLOTS * AT, W)) for c in range(3))
     v0 = jnp.concatenate([pair(g0, turn(g1, AT)), pair(turn(g0, AT), g1)], axis=0)
     v1 = jnp.concatenate([g2, turn(g2, AT)], axis=0)
 
-    lane = iota((2 * SLOTS, W), 1)
-    shares = []
+    shares = [jnp.where(col == PLACE, place, window(v0, v1, Q * y, Q, 0)) for y in range(Y)]
+    sent = dot(route, jnp.concatenate(split(jnp.concatenate(shares, axis=1)), axis=0))
+    at = iota((8, W), 1)
     for y in range(Y):
-        rows = [
-            jnp.where(lane == PLACE + r, place, window(v0, v1, Q * y, Q, Q * r)) for r in range(2)
-        ]
-        shares.append(jnp.concatenate(rows, axis=0))
-    hi, lo = split(jnp.concatenate(shares, axis=1))
-    sent = dot(route, hi) + dot(route, lo)
-    at = iota((2 * 8, W), 1)
-    for y in range(Y):
-        extra = jnp.concatenate(
-            [window(x0, x1, Q * y + Q // 2 * h, Q // 2, POS) for h in range(2)], axis=0
-        )
-        extra = jnp.where(at == SCALAR, energy, extra)
-        share = sent[:, W * y : W * (y + 1)].reshape(XC, Z, W)
+        extra = jnp.where(at == SCALAR, energy, window(x0, x1, Q * y, Q, AT))
         for k in range(XC):
-            out[k * Y + YS.index(y)] = jnp.where(at < POS, share[k], extra)
-
-
-def me():
-    return ((lax.axis_index("x") - X0) & (X - 1)) * C + (lax.axis_index("c") ^ C0)
-
-
-def turn_kernel(got, out, pos):
-    for k in range(XC):
-        s = (got[k * Y] + got[k * Y + 1]) + (got[k * Y + 2] + got[k * Y + 3])
-        out[:, k, :] = s
-    mine = [got[me() * Y + YS.index(y)] for y in range(Y)]
-    a = jnp.concatenate([m[:8] for m in mine], axis=0)
-    b = jnp.concatenate([m[8:] for m in mine], axis=0)
-    a, b = turn(a, -POS), turn(b, Q // 2 - POS)
-    lane = iota(a.shape, 1)
-    pos[...] = jnp.where(lane < Q // 2, a, jnp.where(lane < Q, b, 0.0))
-
-
-def block_kernel(got, pos, out):
+            share = sent[8 * k : 8 * (k + 1), W * y : W * (y + 1)]
+            out[k * Y + YS.index(y)] = pair(share, extra)
+
+
+def turn_kernel(got, out):
+    s = jnp.concatenate(
+        [
+            (got[k * Y] + got[k * Y + 1]) + (got[k * Y + 2] + got[k * Y + 3])
+            for k in range(XC)
+        ],
+        axis=0,
+    )
+    row, col = iota(s.shape, 0), iota(s.shape, 1)
+    place = s[:, PLACE : PLACE + 1].astype(i32)
+    z, place = place >> 10, (place & 1023).astype(f32)
+    e = (((row >> 3) == (col & 7)) & (z == (col >> 3))).astype(f32)
+    before = (iota((64, 64), 1) < iota((64, 64), 0)).astype(f32).astype(bf16)
+    count = dot(before, e.astype(bf16))
+    route = jnp.concatenate([jnp.where(count == r, e, 0.0) for r in (0.0, 1.0)], axis=0)
+    route = route.astype(bf16)
+    low = jnp.where(col < Q, s, jnp.where(col == PLACE, place, 0.0))
+    hi, lo = split(jnp.concatenate([low, turn(low, AT)], axis=0))
+    v = dot(route, hi, ((0,), (0,))) + dot(route, lo, ((0,), (0,)))
+    energy = jnp.sum(jnp.where((row & 7) == 0, s, 0.0), axis=0, keepdims=True)
+    v = jnp.where(iota(v.shape, 1) == SCALAR, energy, v)
+    out[...] = v.reshape(Z, XC, W)
+
+
+def block_kernel(got, first, out):
     v = got[...].reshape(Z * XC, W)
-    lane = iota(v.shape, 1)
-    f = iota((Z * XC, SLOTS), 1).astype(f32) * Y
-    picks, datas = [], []
-    for r in range(2):
-        picks.append((v[:, PLACE + r : PLACE + r + 1] == f).astype(f32).astype(bf16))
-        datas.append(jnp.where(lane < Q, turn(v, -Q * r), 0.0))
+    row, col = iota(v.shape, 0), iota(v.shape, 1)
+    upper = (col >= AT) & (col < AT + Q)
+    f = iota((Z * XC, PLANE * 8), 1).astype(f32) * Y
+    picks = [(v[:, p : p + 1] == f).astype(f32).astype(bf16) for p in (PLACE, AT + PLACE)]
     pick = jnp.concatenate(picks, axis=0)
-    hi, lo = split(jnp.concatenate(datas, axis=0))
+    data = jnp.concatenate([jnp.where(upper, d, 0.0) for d in (turn(v, AT), v)], axis=0)
+    hi, lo = split(data)
     block = dot(pick, hi, ((0,), (0,))) + dot(pick, lo, ((0,), (0,)))
-    virial = -jnp.sum(block * pos[...]) / 3.0
-    energy = jnp.sum(jnp.where(lane == SCALAR, v, 0.0)) / (Z * PLANE)
+    virial = -jnp.sum(block * first[...].reshape(block.shape)) / 3.0
+    energy = jnp.sum(jnp.where(((row & 7) == 0) & (col == SCALAR), v, 0.0)) / (Z * PLANE)
     at = iota(block.shape, 1)
+    lower = turn(pltpu.roll(block, PLANE * 8 - 4, 0), -Q)
+    block = jnp.where(at < AT, lower, block)
     block = jnp.where(at == SCALAR, energy, jnp.where(at == SCALAR - 1, virial, block))
-    lower = turn(pltpu.roll(block, SLOTS - 4, 0), Q)
-    block = jnp.where((at < Q) | (at >= 2 * Q), block, lower)
     for k in range(PLANE):
-        y = YS[k % Y]
-        out[k] = block[8 * y : 8 * y + 4]
+        out[k] = block[8 * k : 8 * k + 4]
 
 
 def scalar_kernel(got, scalars):
@@ -177,8 +166,8 @@
     total = jnp.sum(scalars[...], axis=0)
     energy[0] = total[0, SCALAR]
     virial[0] = total[0, SCALAR - 1]
-    mine = [got[me() * Y + YS.index(y)] for y in range(Y)]
-    mine = [jnp.concatenate([m, turn(m, -Q)], axis=0) for m in mine]
+    mine = [sum(got[k * Y + YS.index(y)] for k in range(XC)) for y in range(Y)]
+    mine = [jnp.concatenate([turn(m, -AT), turn(m, Q - AT)], axis=0) for m in mine]
     lane = iota((8, W), 1)
     m1, m2 = turn(mine[1], Q), turn(mine[2], 2 * Q)
     u = jnp.where(lane < Q, mine[0], jnp.where(lane < 2 * Q, m1, m2))
@@ -233,11 +222,9 @@
     )
     scratch = [pltpu.VMEM(a.shape, a.dtype) for a in args] + [pltpu.SemaphoreType.DMA((5 + PARTS,))]
     args = (pltpu.with_memory_space_constraint(a, pltpu.HBM) for a in args)
-    v = call(send_kernel, arr(PLANE, Z, W), 6, scratch, HBM)(*args)
-    v = over_plane(v)
-    v, pos = call(turn_kernel, (arr(Z, XC, W), arr(SLOTS, W)), 1)(v)
-    v = over_z(v)
-    v = call(block_kernel, arr(PLANE, 4, W), 2)(v, pos)
+    first = over_plane(call(send_kernel, arr(PLANE, 8, W), 6, scratch, HBM)(*args))
+    v = over_z(call(turn_kernel, arr(Z, XC, W), 1)(first))
+    v = call(block_kernel, arr(PLANE, 4, W), 2)(v, first)
     v = over_plane(v)
     scalars = over_z(call(scalar_kernel, arr(Z, 1, W), 1)(v))
     outs = (arr(3, 8 * AT), arr(1), arr(1))

time: 64.5 us -> 63.3 us (0.981)
  blocking collectives: 59.5 us -> 58.1 us
    all_to_all x2, blocking collectives: 29 us -> 26.9 us  [over_plane(): lax.all_to_all(v, ('x', 'c', 'y'), 0, 0, axis_index_groups=[order], tiled...]
    all_to_all x2, blocking collectives: 30.5 us -> 31.2 us  [over_z(): return lax.all_to_all(v, 'z', 0, 0, axis_index_groups=[ZS], tiled=True)]
where the time goes in v5:
time: 63.3 us; the launch traced here: 62.6 us
  blocking collectives  58.1 us (92%)
  Pallas kernels  3.9 us (6%)
  between operations  0.65 us (1%)
    all_to_all x2, blocking collectives, over_z(): return lax.all_to_all(v, 'z', 0, 0, axis_index_groups=[ZS], tiled=True)  31.2 us
    all_to_all x2, blocking collectives, over_plane(): lax.all_to_all(v, ('x', 'c', 'y'), 0, 0, axis_index_groups=[order], tiled...  26.9 us
    pallas_call x1, Pallas kernels, on_device(): call(send_kernel, arr(PLANE, 8, W), 6, scratch, HBM)(*args)  2.14 us

profile of v5, /device:TPU:1, one launch (start us, length us, event | category | flops | bytes accessed | tf_op | source)
XLA Modules:
  0.0 62.6 jit_solution(1239794346412956972)
XLA Ops:
  0.6 2.1 %shard_map.85 = f32[32,8,128]{2,1,0:T(8,128)S(1)} custom-call(bf16[32,3,64,128]{3,2,1,0:T(8,128)(2,1)} %bitcast.5, bf16[32,64]{1,0:T(8,128)(2,1)} %h_dens.1, bf16[32,64]{1,0:T(8,128)(2,1)} %h_terms.1, s32[2,32]{1,0:T(2,128)} %bitcast.6, s32[2,32]{1,0:T(2,128)} %bitcast.7, f32[3,512]{1,0:T(4,128)} %h_pos.1), custom_call_target="tpu_custom_call" | custom-call | flops 20000000 | bytes 262144 | tf_op jit(solution)/shard_map/pallas_call | solution.py:225
  2.8 16.2 %all_to_all.20.got.first = f32[32,8,128]{2,1,0:T(8,128)S(1)} all-to-all(f32[32,8,128]{2,1,0:T(8,128)S(1)} %shard_map.85), channel_id=1, replica_groups={{262,263,260,261,258,259,256,257,390,391,388,389,386,387,384,385,6,7,4,..., dimensions={0} | all-to-all | bytes 262144 | tf_op jit(solution)/shard_map/all_to_all | solution.py:211
  19.0 0.4 shard_map.86
  19.4 18.3 %all_to_all.21.got = f32[16,8,128]{2,1,0:T(8,128)S(1)} all-to-all(f32[16,8,128]{2,1,0:T(8,128)S(1)} %shard_map.86), channel_id=1, replica_groups={{64,72,80,88,96,104,112,120,0,8,16,24,32,40,48,56},{65,73,81,89,97,105,..., dimensions={0} | all-to-all | bytes 131072 | tf_op jit(solution)/shard_map/all_to_all | solution.py:206
  37.7 0.5 shard_map.87
  38.2 10.7 %all_to_all.22.got = f32[32,4,128]{2,1,0:T(4,128)S(1)} all-to-all(f32[32,4,128]{2,1,0:T(4,128)S(1)} %shard_map.87), channel_id=1, replica_groups={{262,263,260,261,258,259,256,257,390,391,388,389,386,387,384,385,6,7,4,..., dimensions={0} | all-to-all | bytes 131072 | tf_op jit(solution)/shard_map/all_to_all | solution.py:211
  48.9 12.9 %all_to_all.23.scalars = f32[16,1,128]{2,1,0:T(1,128)S(1)} all-to-all(f32[16,1,128]{2,1,0:T(1,128)S(1)} %shard_map.88), channel_id=1, replica_groups={{64,72,80,88,96,104,112,120,0,8,16,24,32,40,48,56},{65,73,81,89,97,105,..., dimensions={0} | all-to-all | bytes 16384 | tf_op jit(solution)/shard_map/all_to_all | solution.py:206
  61.8 0.8 %shard_map.89 = (f32[3,512]{1,0:T(4,128)}, f32[1]{0:T(128)}, f32[1]{0:T(128)}) custom-call(f32[32,4,128]{2,1,0:T(4,128)S(1)} %all_to_all.22.got, f32[16,1,128]{2,1,0:T(1,128)S(1)} %all_to_all.23.scalars), custom_call_target="tpu_custom_call" | custom-call | flops 20000000 | bytes 262144 | tf_op jit(solution)/shard_map/pallas_call | solution.py:231
  (1 shorter events, 0.0 us)

commit v6 on v5

--- a/solution.py
+++ b/solution.py
@@ -78,8 +78,9 @@
     key = ((z * 8 + xc) * SLOTS + f) * (2 * SLOTS) + (col[:1] & (2 * SLOTS - 1))
     key_of = jnp.sum(jnp.where(row == col, key.astype(f32), 0.0), axis=1, keepdims=True)
     turn_of = jnp.sum((key_of < key.astype(f32)).astype(f32), axis=0, keepdims=True).astype(i32)
-    route = (row == (turn_of & 7) * 8 + (turn_of >> 3)).astype(f32).astype(bf16)
-    place = (key_of.astype(i32) >> 6).astype(f32)
+    chosen = (row == (turn_of & 7) * 8 + (turn_of >> 3)) & (col < 2 * SLOTS)
+    place = jnp.sum(jnp.where(chosen, (key >> 6).astype(f32), 0.0), axis=1, keepdims=True)
+    second = jnp.sum(jnp.where(chosen & (col >= SLOTS), 1.0, 0.0), axis=1, keepdims=True) > 0
 
     lines = []
     for f in range(8):
@@ -92,25 +93,25 @@
     d = dens[...].astype(f32)
     energy = jnp.sum(d * terms[...].astype(f32))
     dd = jnp.concatenate([d, d], axis=1)
-    row, half = iota(dd.shape, 0), iota(dd.shape, 1) // AT
+    side, half = iota(dd.shape, 0), iota(dd.shape, 1) // AT
     diag = jnp.concatenate(
-        [jnp.where(row == 2 * j + half, dd, 0.0).astype(bf16) for j in range(SLOTS // 2)], axis=1
-    )
+        [jnp.where(side == 2 * j + half, dd, 0.0).astype(bf16) for j in range(SLOTS // 2)], axis=1
+    )
+    route = chosen.astype(f32).astype(bf16)[:, : 2 * SLOTS]
+    weights = dot(route, jnp.concatenate([diag, diag], axis=0)).astype(bf16)
 
     for copy in copies[-PARTS:]:
         copy.wait()
-    g0, g1, g2 = (dot(diag, ints[:, c].reshape(SLOTS * AT, W)) for c in range(3))
-    v0 = jnp.concatenate([pair(g0, turn(g1, AT)), pair(turn(g0, AT), g1)], axis=0)
-    v1 = jnp.concatenate([g2, turn(g2, AT)], axis=0)
-
+    g = [dot(weights, ints[:, c].reshape(SLOTS * AT, W)) for c in range(3)]
+    h = [turn(v, AT) for v in g]
+    v0 = pair(jnp.where(second, h[0], g[0]), jnp.where(second, g[1], h[1]))
+    v1 = jnp.where(second, h[2], g[2])
     shares = [jnp.where(col == PLACE, place, window(v0, v1, Q * y, Q, 0)) for y in range(Y)]
-    sent = dot(route, jnp.concatenate(split(jnp.concatenate(shares, axis=1)), axis=0))
     at = iota((8, W), 1)
     for y in range(Y):
         extra = jnp.where(at == SCALAR, energy, window(x0, x1, Q * y, Q, AT))
         for k in range(XC):
-            share = sent[8 * k : 8 * (k + 1), W * y : W * (y + 1)]
-            out[k * Y + YS.index(y)] = pair(share, extra)
+            out[k * Y + YS.index(y)] = pair(shares[y][8 * k : 8 * (k + 1)], extra)
 
 
 def turn_kernel(got, out):
@@ -124,10 +125,10 @@
     row, col = iota(s.shape, 0), iota(s.shape, 1)
     place = s[:, PLACE : PLACE + 1].astype(i32)
     z, place = place >> 10, (place & 1023).astype(f32)
-    e = (((row >> 3) == (col & 7)) & (z == (col >> 3))).astype(f32)
-    before = (iota((64, 64), 1) < iota((64, 64), 0)).astype(f32).astype(bf16)
-    count = dot(before, e.astype(bf16))
-    route = jnp.concatenate([jnp.where(count == r, e, 0.0) for r in (0.0, 1.0)], axis=0)
+    e = ((row >> 3) == (col & 7)) & (z == (col >> 3))
+    z = jnp.broadcast_to(z, s.shape)
+    again = (z == pltpu.roll(z, 1, 0)) & ((row & 7) != 0)
+    route = jnp.concatenate([(e & ~again).astype(f32), (e & again).astype(f32)], axis=0)
     route = route.astype(bf16)
     low = jnp.where(col < Q, s, jnp.where(col == PLACE, place, 0.0))
     hi, lo = split(jnp.concatenate([low, turn(low, AT)], axis=0))
@@ -148,7 +149,7 @@
     hi, lo = split(data)
     block = dot(pick, hi, ((0,), (0,))) + dot(pick, lo, ((0,), (0,)))
     virial = -jnp.sum(block * first[...].reshape(block.shape)) / 3.0
-    energy = jnp.sum(jnp.where(((row & 7) == 0) & (col == SCALAR), v, 0.0)) / (Z * PLANE)
+    energy = jnp.sum(jnp.where((row & 7) == 0, v, 0.0), axis=0, keepdims=True) / (Z * PLANE)
     at = iota(block.shape, 1)
     lower = turn(pltpu.roll(block, PLANE * 8 - 4, 0), -Q)
     block = jnp.where(at < AT, lower, block)

time: 63.3 us -> 63.1 us (level)
  no operation moved by 1% of the time
where the time goes in v6:
time: 63.1 us; the launch traced here: 62.4 us
  blocking collectives  58.1 us (92%)
  Pallas kernels  3.67 us (6%)
  between operations  0.65 us (1%)
    all_to_all x2, blocking collectives, over_z(): return lax.all_to_all(v, 'z', 0, 0, axis_index_groups=[ZS], tiled=True)  31.2 us
    all_to_all x2, blocking collectives, over_plane(): lax.all_to_all(v, ('x', 'c', 'y'), 0, 0, axis_index_groups=[order], tiled...  26.9 us
    pallas_call x1, Pallas kernels, on_device(): call(send_kernel, arr(PLANE, 8, W), 6, scratch, HBM)(*args)  2.02 us

profile of v6, /device:TPU:1, one launch (start us, length us, event | category | flops | bytes accessed | tf_op | source)
XLA Modules:
  0.0 62.4 jit_solution(16598402839435514936)
XLA Ops:
  0.6 2.0 %shard_map.85 = f32[32,8,128]{2,1,0:T(8,128)S(1)} custom-call(bf16[32,3,64,128]{3,2,1,0:T(8,128)(2,1)} %bitcast.5, bf16[32,64]{1,0:T(8,128)(2,1)} %h_dens.1, bf16[32,64]{1,0:T(8,128)(2,1)} %h_terms.1, s32[2,32]{1,0:T(2,128)} %bitcast.6, s32[2,32]{1,0:T(2,128)} %bitcast.7, f32[3,512]{1,0:T(4,128)} %h_pos.1), custom_call_target="tpu_custom_call" | custom-call | flops 20000000 | bytes 262144 | tf_op jit(solution)/shard_map/pallas_call | solution.py:226
  2.7 16.2 %all_to_all.20.got.first = f32[32,8,128]{2,1,0:T(8,128)S(1)} all-to-all(f32[32,8,128]{2,1,0:T(8,128)S(1)} %shard_map.85), channel_id=1, replica_groups={{262,263,260,261,258,259,256,257,390,391,388,389,386,387,384,385,6,7,4,..., dimensions={0} | all-to-all | bytes 262144 | tf_op jit(solution)/shard_map/all_to_all | solution.py:212
  18.9 0.3 shard_map.86
  19.2 18.3 %all_to_all.21.got = f32[16,8,128]{2,1,0:T(8,128)S(1)} all-to-all(f32[16,8,128]{2,1,0:T(8,128)S(1)} %shard_map.86), channel_id=1, replica_groups={{64,72,80,88,96,104,112,120,0,8,16,24,32,40,48,56},{65,73,81,89,97,105,..., dimensions={0} | all-to-all | bytes 131072 | tf_op jit(solution)/shard_map/all_to_all | solution.py:207
  37.5 0.5 shard_map.87
  38.0 10.7 %all_to_all.22.got = f32[32,4,128]{2,1,0:T(4,128)S(1)} all-to-all(f32[32,4,128]{2,1,0:T(4,128)S(1)} %shard_map.87), channel_id=1, replica_groups={{262,263,260,261,258,259,256,257,390,391,388,389,386,387,384,385,6,7,4,..., dimensions={0} | all-to-all | bytes 131072 | tf_op jit(solution)/shard_map/all_to_all | solution.py:212
  48.7 12.9 %all_to_all.23.scalars = f32[16,1,128]{2,1,0:T(1,128)S(1)} all-to-all(f32[16,1,128]{2,1,0:T(1,128)S(1)} %shard_map.88), channel_id=1, replica_groups={{64,72,80,88,96,104,112,120,0,8,16,24,32,40,48,56},{65,73,81,89,97,105,..., dimensions={0} | all-to-all | bytes 16384 | tf_op jit(solution)/shard_map/all_to_all | solution.py:207
  61.6 0.8 %shard_map.89 = (f32[3,512]{1,0:T(4,128)}, f32[1]{0:T(128)}, f32[1]{0:T(128)}) custom-call(f32[32,4,128]{2,1,0:T(4,128)S(1)} %all_to_all.22.got, f32[16,1,128]{2,1,0:T(1,128)S(1)} %all_to_all.23.scalars), custom_call_target="tpu_custom_call" | custom-call | flops 20000000 | bytes 262144 | tf_op jit(solution)/shard_map/pallas_call | solution.py:232
  (1 shorter events, 0.0 us)

commit v7 on v6

--- a/solution.py
+++ b/solution.py
@@ -15,7 +15,7 @@
 Q = 48
 PARTS = 4
 PLACE, SCALAR = Q, 127
-X0, C0, Y0, Z0 = 2, 1, 2, 8
+X0, C0, Y0, Z0 = 2, 1, 2, 9
 ZS = [(Z0 + k) % Z for k in range(Z)]
 YS = [(Y0 + k) % Y for k in range(Y)]
 XCS = [(X0 + i) % X * C + (C0 + j) % C for i in range(X) for j in range(C)]
@@ -125,14 +125,16 @@
     row, col = iota(s.shape, 0), iota(s.shape, 1)
     place = s[:, PLACE : PLACE + 1].astype(i32)
     z, place = place >> 10, (place & 1023).astype(f32)
-    e = ((row >> 3) == (col & 7)) & (z == (col >> 3))
     z = jnp.broadcast_to(z, s.shape)
     again = (z == pltpu.roll(z, 1, 0)) & ((row & 7) != 0)
-    route = jnp.concatenate([(e & ~again).astype(f32), (e & again).astype(f32)], axis=0)
-    route = route.astype(bf16)
+    to = z * XC + (row >> 3) + jnp.where(again, Z * XC, 0)
+    to = jnp.where(row == (col & 63), to.astype(f32), 0.0)
+    to = jnp.sum(to, axis=0, keepdims=True).astype(i32)
+    r, c = iota((Z * XC, W), 0), iota((Z * XC, W), 1)
+    route = (r + jnp.where(c < 64, 0, Z * XC) == to).astype(f32).astype(bf16)
     low = jnp.where(col < Q, s, jnp.where(col == PLACE, place, 0.0))
     hi, lo = split(jnp.concatenate([low, turn(low, AT)], axis=0))
-    v = dot(route, hi, ((0,), (0,))) + dot(route, lo, ((0,), (0,)))
+    v = dot(route, hi) + dot(route, lo)
     energy = jnp.sum(jnp.where((row & 7) == 0, s, 0.0), axis=0, keepdims=True)
     v = jnp.where(iota(v.shape, 1) == SCALAR, energy, v)
     out[...] = v.reshape(Z, XC, W)
@@ -142,12 +144,15 @@
     v = got[...].reshape(Z * XC, W)
     row, col = iota(v.shape, 0), iota(v.shape, 1)
     upper = (col >= AT) & (col < AT + Q)
-    f = iota((Z * XC, PLANE * 8), 1).astype(f32) * Y
-    picks = [(v[:, p : p + 1] == f).astype(f32).astype(bf16) for p in (PLACE, AT + PLACE)]
-    pick = jnp.concatenate(picks, axis=0)
+    f = iota((PLANE * 8, W), 0).astype(f32) * Y
+    picks = []
+    for p in (PLACE, AT + PLACE):
+        place = jnp.sum(jnp.where(row == col, v[:, p : p + 1], 0.0), axis=0, keepdims=True)
+        picks.append((place == f).astype(f32).astype(bf16))
+    pick = jnp.concatenate(picks, axis=1)
     data = jnp.concatenate([jnp.where(upper, d, 0.0) for d in (turn(v, AT), v)], axis=0)
     hi, lo = split(data)
-    block = dot(pick, hi, ((0,), (0,))) + dot(pick, lo, ((0,), (0,)))
+    block = dot(pick, hi) + dot(pick, lo)
     virial = -jnp.sum(block * first[...].reshape(block.shape)) / 3.0
     energy = jnp.sum(jnp.where((row & 7) == 0, v, 0.0), axis=0, keepdims=True) / (Z * PLANE)
     at = iota(block.shape, 1)

time: 63.1 us -> 63 us (level)
  no operation moved by 1% of the time
where the time goes in v7:
time: 63 us; the launch traced here: 62.3 us
  blocking collectives  58 us (92%)
  Pallas kernels  3.64 us (6%)
  between operations  0.65 us (1%)
    all_to_all x2, blocking collectives, over_z(): return lax.all_to_all(v, 'z', 0, 0, axis_index_groups=[ZS], tiled=True)  30.7 us
    all_to_all x2, blocking collectives, over_plane(): lax.all_to_all(v, ('x', 'c', 'y'), 0, 0, axis_index_groups=[order], tiled...  27.3 us
    pallas_call x1, Pallas kernels, on_device(): call(send_kernel, arr(PLANE, 8, W), 6, scratch, HBM)(*args)  2.02 us

profile of v7, /device:TPU:1, one launch (start us, length us, event | category | flops | bytes accessed | tf_op | source)
XLA Modules:
  0.0 62.3 jit_solution(11031825022617495743)
XLA Ops:
  0.6 2.0 %shard_map.85 = f32[32,8,128]{2,1,0:T(8,128)S(1)} custom-call(bf16[32,3,64,128]{3,2,1,0:T(8,128)(2,1)} %bitcast.5, bf16[32,64]{1,0:T(8,128)(2,1)} %h_dens.1, bf16[32,64]{1,0:T(8,128)(2,1)} %h_terms.1, s32[2,32]{1,0:T(2,128)} %bitcast.6, s32[2,32]{1,0:T(2,128)} %bitcast.7, f32[3,512]{1,0:T(4,128)} %h_pos.1), custom_call_target="tpu_custom_call" | custom-call | flops 20000000 | bytes 262144 | tf_op jit(solution)/shard_map/pallas_call | solution.py:231
  2.7 16.2 %all_to_all.20.got.first = f32[32,8,128]{2,1,0:T(8,128)S(1)} all-to-all(f32[32,8,128]{2,1,0:T(8,128)S(1)} %shard_map.85), channel_id=1, replica_groups={{262,263,260,261,258,259,256,257,390,391,388,389,386,387,384,385,6,7,4,..., dimensions={0} | all-to-all | bytes 262144 | tf_op jit(solution)/shard_map/all_to_all | solution.py:217
  18.9 0.3 shard_map.86
  19.2 17.9 %all_to_all.21.got = f32[16,8,128]{2,1,0:T(8,128)S(1)} all-to-all(f32[16,8,128]{2,1,0:T(8,128)S(1)} %shard_map.86), channel_id=1, replica_groups={{72,80,88,96,104,112,120,0,8,16,24,32,40,48,56,64},{73,81,89,97,105,113..., dimensions={0} | all-to-all | bytes 131072 | tf_op jit(solution)/shard_map/all_to_all | solution.py:212
  37.1 0.5 shard_map.87
  37.5 11.1 %all_to_all.22.got = f32[32,4,128]{2,1,0:T(4,128)S(1)} all-to-all(f32[32,4,128]{2,1,0:T(4,128)S(1)} %shard_map.87), channel_id=1, replica_groups={{262,263,260,261,258,259,256,257,390,391,388,389,386,387,384,385,6,7,4,..., dimensions={0} | all-to-all | bytes 131072 | tf_op jit(solution)/shard_map/all_to_all | solution.py:217
  48.7 12.9 %all_to_all.23.scalars = f32[16,1,128]{2,1,0:T(1,128)S(1)} all-to-all(f32[16,1,128]{2,1,0:T(1,128)S(1)} %shard_map.88), channel_id=1, replica_groups={{72,80,88,96,104,112,120,0,8,16,24,32,40,48,56,64},{73,81,89,97,105,113..., dimensions={0} | all-to-all | bytes 16384 | tf_op jit(solution)/shard_map/all_to_all | solution.py:212
  61.5 0.8 %shard_map.89 = (f32[3,512]{1,0:T(4,128)}, f32[1]{0:T(128)}, f32[1]{0:T(128)}) custom-call(f32[32,4,128]{2,1,0:T(4,128)S(1)} %all_to_all.22.got, f32[16,1,128]{2,1,0:T(1,128)S(1)} %all_to_all.23.scalars), custom_call_target="tpu_custom_call" | custom-call | flops 20000000 | bytes 262144 | tf_op jit(solution)/shard_map/pallas_call | solution.py:237
  (1 shorter events, 0.0 us)

commit v8 on v7

--- a/solution.py
+++ b/solution.py
@@ -15,8 +15,9 @@
 Q = 48
 PARTS = 4
 PLACE, SCALAR = Q, 127
-X0, C0, Y0, Z0 = 2, 1, 2, 9
+X0, C0, Y0, Z0, Z2 = 2, 1, 2, 10, 9
 ZS = [(Z0 + k) % Z for k in range(Z)]
+Z2S = [(Z2 + k) % Z for k in range(Z)]
 YS = [(Y0 + k) % Y for k in range(Y)]
 XCS = [(X0 + i) % X * C + (C0 + j) % C for i in range(X) for j in range(C)]
 DIMER = ("x", "z", "c")
@@ -208,8 +209,8 @@
     return jax.ShapeDtypeStruct(shape, f32)
 
 
-def over_z(v):
-    return lax.all_to_all(v, "z", 0, 0, axis_index_groups=[ZS], tiled=True)
+def over_z(v, order):
+    return lax.all_to_all(v, "z", 0, 0, axis_index_groups=[order], tiled=True)
 
 
 def over_plane(v):
@@ -229,10 +230,10 @@
     scratch = [pltpu.VMEM(a.shape, a.dtype) for a in args] + [pltpu.SemaphoreType.DMA((5 + PARTS,))]
     args = (pltpu.with_memory_space_constraint(a, pltpu.HBM) for a in args)
     first = over_plane(call(send_kernel, arr(PLANE, 8, W), 6, scratch, HBM)(*args))
-    v = over_z(call(turn_kernel, arr(Z, XC, W), 1)(first))
+    v = over_z(call(turn_kernel, arr(Z, XC, W), 1)(first), ZS)
     v = call(block_kernel, arr(PLANE, 4, W), 2)(v, first)
     v = over_plane(v)
-    scalars = over_z(call(scalar_kernel, arr(Z, 1, W), 1)(v))
+    scalars = over_z(call(scalar_kernel, arr(Z, 1, W), 1)(v), Z2S)
     outs = (arr(3, 8 * AT), arr(1), arr(1))
     forces, energy, virial = call(force_kernel, outs, 2, spaces=(VM, SM, SM))(v, scalars)
     return forces, energy.reshape(()), virial.reshape(())

time: 63 us -> 63.1 us (level)
  no operation moved by 1% of the time
where the time goes in v8:
time: 63.1 us; the launch traced here: 62.4 us
  blocking collectives  58.1 us (92%)
  Pallas kernels  3.64 us (6%)
  between operations  0.65 us (1%)
    all_to_all x2, blocking collectives, over_z(): return lax.all_to_all(v, 'z', 0, 0, axis_index_groups=[order], tiled=True)  30.8 us
    all_to_all x2, blocking collectives, over_plane(): lax.all_to_all(v, ('x', 'c', 'y'), 0, 0, axis_index_groups=[order], tiled...  27.3 us
    pallas_call x1, Pallas kernels, on_device(): call(send_kernel, arr(PLANE, 8, W), 6, scratch, HBM)(*args)  2.02 us

profile of v8, /device:TPU:1, one launch (start us, length us, event | category | flops | bytes accessed | tf_op | source)
XLA Modules:
  0.0 62.4 jit_solution(2648965738343314945)
XLA Ops:
  0.6 2.0 %shard_map.85 = f32[32,8,128]{2,1,0:T(8,128)S(1)} custom-call(bf16[32,3,64,128]{3,2,1,0:T(8,128)(2,1)} %bitcast.5, bf16[32,64]{1,0:T(8,128)(2,1)} %h_dens.1, bf16[32,64]{1,0:T(8,128)(2,1)} %h_terms.1, s32[2,32]{1,0:T(2,128)} %bitcast.6, s32[2,32]{1,0:T(2,128)} %bitcast.7, f32[3,512]{1,0:T(4,128)} %h_pos.1), custom_call_target="tpu_custom_call" | custom-call | flops 20000000 | bytes 262144 | tf_op jit(solution)/shard_map/pallas_call | solution.py:232
  2.7 16.2 %all_to_all.20.got.first = f32[32,8,128]{2,1,0:T(8,128)S(1)} all-to-all(f32[32,8,128]{2,1,0:T(8,128)S(1)} %shard_map.85), channel_id=1, replica_groups={{262,263,260,261,258,259,256,257,390,391,388,389,386,387,384,385,6,7,4,..., dimensions={0} | all-to-all | bytes 262144 | tf_op jit(solution)/shard_map/all_to_all | solution.py:218
  18.9 0.3 shard_map.86
  19.2 17.8 %all_to_all.21.got = f32[16,8,128]{2,1,0:T(8,128)S(1)} all-to-all(f32[16,8,128]{2,1,0:T(8,128)S(1)} %shard_map.86), channel_id=1, replica_groups={{80,88,96,104,112,120,0,8,16,24,32,40,48,56,64,72},{81,89,97,105,113,12..., dimensions={0} | all-to-all | bytes 131072 | tf_op jit(solution)/shard_map/all_to_all | solution.py:213
  37.0 0.5 shard_map.87
  37.5 11.1 %all_to_all.22.got = f32[32,4,128]{2,1,0:T(4,128)S(1)} all-to-all(f32[32,4,128]{2,1,0:T(4,128)S(1)} %shard_map.87), channel_id=1, replica_groups={{262,263,260,261,258,259,256,257,390,391,388,389,386,387,384,385,6,7,4,..., dimensions={0} | all-to-all | bytes 131072 | tf_op jit(solution)/shard_map/all_to_all | solution.py:218
  48.6 13.0 %all_to_all.23.scalars = f32[16,1,128]{2,1,0:T(1,128)S(1)} all-to-all(f32[16,1,128]{2,1,0:T(1,128)S(1)} %shard_map.88), channel_id=1, replica_groups={{72,80,88,96,104,112,120,0,8,16,24,32,40,48,56,64},{73,81,89,97,105,113..., dimensions={0} | all-to-all | bytes 16384 | tf_op jit(solution)/shard_map/all_to_all | solution.py:213
  61.6 0.8 %shard_map.89 = (f32[3,512]{1,0:T(4,128)}, f32[1]{0:T(128)}, f32[1]{0:T(128)}) custom-call(f32[32,4,128]{2,1,0:T(4,128)S(1)} %all_to_all.22.got, f32[16,1,128]{2,1,0:T(1,128)S(1)} %all_to_all.23.scalars), custom_call_target="tpu_custom_call" | custom-call | flops 20000000 | bytes 262144 | tf_op jit(solution)/shard_map/pallas_call | solution.py:238
  (1 shorter events, 0.0 us)
